TPU v7x, 32 devices: a 4x4x1 block of a 4x4x8 slice. The times are simulated.
32 devices in a mesh: dp: 1 (over z), sp: 32 (over y, x, core).
Axes of the slice: x: 4, y: 4, z: 1, core: 2. Of those that a mesh axis runs over, the one named last changes fastest.
The devices are a block of a 4x4x8 slice.
Arguments:
- tokens: bfloat16 [2, 8192, 2048], P('dp', 'sp')
- expert_ids: int32 [2, 8192, 8], P('dp', 'sp')
- w_query: bfloat16 [2048, 32, 128], replicated
- w_key: bfloat16 [2048, 4, 128], replicated
- w_value: bfloat16 [2048, 4, 128], replicated
- w_out: bfloat16 [32, 128, 2048], replicated
- w_router: bfloat16 [2048, 128], replicated
Outputs:
- output 1: bfloat16 [2, 8192, 2048], P('dp', 'sp')
- output 2: bfloat16 [2, 128, 1024, 2048], P('dp', 'sp')
All inputs are finite; a program needn't handle non-finite values.
Results may differ from a plain program's by a relative error of at most 0.0135601.
Values are sent between devices in bfloat16 or wider.
A program may use at most 768 MiB of HBM per device.

v0:
```python
import math
import jax
import jax.numpy as jnp
from jax import lax
from jax.sharding import PartitionSpec as P


def causal_attention(queries, key_rows, value_rows, q_offset):
    n_micro, q_len, kv_local, group_q, head_dim = queries.shape
    k_len = key_rows.shape[1]
    q_block = min(q_len, 128)
    key_pos = jnp.arange(k_len)

    def one_block(blk_start):
        q_blk = lax.dynamic_slice_in_dim(queries, blk_start, q_block, axis=1)
        scores = jnp.einsum('mqhgd,mkhd->mhgqk', q_blk, key_rows, preferred_element_type=jnp.float32) / math.sqrt(head_dim)
        q_pos = q_offset + blk_start + jnp.arange(q_block)
        scores = jnp.where(q_pos[:, None] >= key_pos[None, :], scores, -jnp.inf)
        attn_probs = jax.nn.softmax(scores, axis=-1).astype(jnp.bfloat16)
        block_out = jnp.einsum('mhgqk,mkhd->mqhgd', attn_probs, value_rows, preferred_element_type=jnp.float32)
        return block_out.astype(jnp.bfloat16)

    blocks = lax.map(one_block, jnp.arange(q_len // q_block) * q_block)
    return jnp.moveaxis(blocks, 0, 1).reshape(n_micro, q_len, kv_local, group_q, head_dim)


def route_rows(hidden, expert_ids, w_router, capacity):
    n_micro, tok_dev, top_k = expert_ids.shape
    experts = w_router.shape[1]
    logits = jnp.einsum('mtd,de->mte', hidden, w_router, preferred_element_type=jnp.float32)
    pair_hot = (expert_ids[..., None] == jnp.arange(experts)).astype(jnp.int32)
    expert_f32 = pair_hot.astype(jnp.float32)
    chosen = jnp.sum(expert_f32 * logits[:, :, None, :], axis=-1)
    gate_w = jax.nn.softmax(chosen, axis=-1)
    flat_hot = pair_hot.reshape(n_micro, tok_dev * top_k, experts)
    slot_rank = jnp.sum((jnp.cumsum(flat_hot, axis=1) - flat_hot) * flat_hot, axis=-1).reshape(n_micro, tok_dev, top_k)
    rank_hot = slot_rank[..., None] == jnp.arange(capacity)
    select = jnp.einsum('mtke,mtkc->mtec', pair_hot.astype(jnp.bfloat16), rank_hot.astype(jnp.bfloat16), preferred_element_type=jnp.float32).astype(jnp.bfloat16)
    slot_gate = jnp.einsum('mtke,mtkc->mec', expert_f32 * gate_w[..., None], rank_hot.astype(jnp.float32), preferred_element_type=jnp.float32, precision=lax.Precision.HIGHEST)
    gathered = jnp.einsum('mtec,mtd->mecd', select, hidden, preferred_element_type=jnp.float32)
    return (gathered * slot_gate[..., None]).astype(jnp.bfloat16)


def solution(mesh):
    groups = mesh.shape['sp']

    def local_step(tokens, expert_ids, w_query, w_key, w_value, w_out, w_router):
        n_micro = tokens.shape[0]
        tok_dev = tokens.shape[1]
        top_k = expert_ids.shape[2]
        head_dim = w_query.shape[2]
        kv_all = w_key.shape[1]
        experts = w_router.shape[1]
        capacity = 2 * tok_dev * top_k // experts
        repeat = max(groups // kv_all, 1)
        queries = jnp.einsum('mtd,dhk->mthk', tokens, w_query, preferred_element_type=jnp.float32).astype(jnp.bfloat16)
        key_rows = jnp.einsum('mtd,dhk->mthk', tokens, w_key, preferred_element_type=jnp.float32).astype(jnp.bfloat16)
        value_rows = jnp.einsum('mtd,dhk->mthk', tokens, w_value, preferred_element_type=jnp.float32).astype(jnp.bfloat16)
        if repeat > 1:
            key_rows = jnp.repeat(key_rows, repeat, axis=2)
            value_rows = jnp.repeat(value_rows, repeat, axis=2)
        queries = lax.all_to_all(queries, 'sp', 2, 1, tiled=True)
        key_rows = lax.all_to_all(key_rows, 'sp', 2, 1, tiled=True)
        value_rows = lax.all_to_all(value_rows, 'sp', 2, 1, tiled=True)
        seq_len, heads_local = queries.shape[1], queries.shape[2]
        kv_local = key_rows.shape[2]
        queries = queries.reshape(n_micro, seq_len, kv_local, heads_local // kv_local, head_dim)
        attn_out = causal_attention(queries, key_rows, value_rows, 0).reshape(n_micro, seq_len, heads_local, head_dim)
        attn_out = lax.all_to_all(attn_out, 'sp', 1, 2, tiled=True)
        attn_proj = jnp.einsum('mthk,hkd->mtd', attn_out, w_out, preferred_element_type=jnp.float32)
        hidden = (tokens.astype(jnp.float32) + attn_proj).astype(jnp.bfloat16)
        send_rows = route_rows(hidden, expert_ids, w_router, capacity)
        recv_rows = lax.all_to_all(send_rows, 'sp', 1, 2, tiled=True)
        return hidden, recv_rows

    return jax.shard_map(
        local_step,
        mesh=mesh,
        in_specs=(P('dp', 'sp', None), P('dp', 'sp', None), P(), P(), P(), P(), P()),
        out_specs=(P('dp', 'sp', None), P('dp', 'sp', None, None)),
        check_vma=False,
    )
```

profile of v0, /device:TPU:97, one launch (start us, length us, event | category | flops | bytes accessed | tf_op | source)
XLA Modules:
  0.0 1576.1 jit_solution(12644213141004454280)
XLA Ops:
  7.3 9.1 all-to-all-start.2
  19.3 49.4 %all-to-all-done.2 = bf16[2,256,32,128]{3,1,0,2:T(8,128)(2,1)} async-done(((bf16[2,256,32,128]{3,1,0,2:T(8,128)(2,1)}), bf16[2,256,32,128]{3,1,0,2:T(8,128)(2,1)}, u32[]{:S(2)}, u32[]{:S(2)}) %all-to-all-start.2) | async-done | bytes 4194336 | tf_op jit(solution)/shard_map/all_to_all | solution.py:64
  71.8 7.9 all-to-all-start.1
  79.7 12.6 fusion.39
  94.5 37.3 %all-to-all-done.1 = bf16[2,256,32,128]{3,1,0,2:T(8,128)(2,1)} async-done(((bf16[2,256,32,128]{3,1,0,2:T(8,128)(2,1)}), bf16[2,256,32,128]{3,1,0,2:T(8,128)(2,1)}, u32[]{:S(2)}, u32[]{:S(2)}) %all-to-all-start.1) | async-done | bytes 4194336 | tf_op jit(solution)/shard_map/all_to_all | solution.py:63
  131.8 8.7 all-to-all-start
  140.5 4.6 copy.50
  145.2 4.7 copy.47
  149.8 45.1 %all-to-all-done = bf16[2,256,32,128]{3,1,0,2:T(8,128)(2,1)} async-done(((bf16[2,256,32,128]{3,1,0,2:T(8,128)(2,1)}), bf16[2,256,32,128]{3,1,0,2:T(8,128)(2,1)}, u32[]{:S(2)}, u32[]{:S(2)}) %all-to-all-start) | async-done | bytes 4194336 | tf_op jit(solution)/shard_map/all_to_all | solution.py:62
  194.9 4.7 copy.44
  199.6 817.0 %while.11 = (s32[]{:T(128)}, bf16[64,2,128,1,1,128]{5,2,0,1,4,3:T(8,128)(2,1)}, s32[64]{0:T(128)S(1)}, bf16[2,8192,1,1,128]{4,1,0,3,2:T(8,128)(2,1)}, bf16[2,819...) while((s32[]{:T(128)}, ...), condition=%wide.region_3.4_spmd.clone, body=%wide.region_0.3_spmd.clone.sunk | while | flops 1091600000 | bytes 52566200 | solution.py:23
  203.3 4.3 fusion.93
  216.1 4.3 fusion.93
  228.8 4.3 fusion.93
  241.6 4.3 fusion.93
  279.9 4.3 fusion.93
  292.7 4.3 fusion.93
  305.4 4.3 fusion.93
  331.0 4.3 fusion.93
  343.7 4.3 fusion.93
  356.5 4.3 fusion.93
  394.8 4.3 fusion.93
  407.6 4.3 fusion.93
  420.3 4.3 fusion.93
  458.6 4.3 fusion.93
  471.4 4.3 fusion.93
  484.2 4.3 fusion.93
  522.5 4.3 fusion.93
  535.2 4.3 fusion.93
  548.0 4.3 fusion.93
  573.5 4.3 fusion.93
  586.3 4.3 fusion.93
  599.1 4.3 fusion.93
  637.4 4.3 fusion.93
  650.1 4.3 fusion.93
  662.9 4.3 fusion.93
  701.2 4.3 fusion.93
  714.0 4.3 fusion.93
  726.7 4.3 fusion.93
  765.0 4.3 fusion.93
  1016.6 10.1 copy.52
  1026.7 6.2 all-to-all-start.3
  1042.5 43.2 %all-to-all-done.3 = bf16[2,8192,1,128]{3,0,2,1:T(2,128)(2,1)} async-done(((bf16[2,8192,1,128]{3,0,2,1:T(2,128)(2,1)}), bf16[2,8192,1,128]{3,0,2,1:T(2,128)(2,1)}, u32[]{:S(2)}, u32[]{:S(2)}) %all-to-all-start.3) | async-done | bytes 4194336 | tf_op jit(solution)/shard_map/all_to_all | solution.py:69
  1088.6 11.6 fusion.33
  1105.4 16.6 %multiply_convert_fusion = bf16[2,128,32,2048]{3,1,2,0:T(8,128)(2,1)} fusion(f32[2,128,32]{1,2,0:T(8,128)S(1)} %fusion.69, bf16[2,256,128,32]{2,3,1,0:T(8,128)(2,1)S(1)} %copy-done.2, bf16[2,256,2048]{2,1,0:T(8,128)(2,1)S(1)} %fusion.33), kind=kOutput, calls=%fused_computation.20 | convolution fusion | flops 8623489024 | bytes 39878656 | tf_op jit(solution)/shard_map/mtec,mtd->mecd/dot_general | solution.py:40
  1122.0 30.0 %copy.62 = bf16[2,128,32,2048]{3,2,0,1:T(8,128)(2,1)} copy(bf16[2,128,32,2048]{3,1,2,0:T(8,128)(2,1)} %multiply_convert_fusion) | data formatting | bytes 67108864 | tf_op jit(solution)/shard_map/convert_element_type | solution.py:41
  1152.0 401.2 %all_to_all.87 = bf16[2,128,32,2048]{3,2,0,1:T(8,128)(2,1)} all-to-all(bf16[2,128,32,2048]{3,2,0,1:T(8,128)(2,1)} %copy.62), channel_id=1, replica_groups=mesh['dp'=1,'sp'=32] {'sp'}, dimensions={1} | all-to-all | bytes 67108864 | tf_op jit(solution)/shard_map/all_to_all | solution.py:73
  1553.2 22.9 %copy.63 = bf16[2,4,32,32,2048]{4,3,2,1,0:T(8,128)(2,1)} copy(bf16[2,4,32,32,2048]{4,3,0,1,2:T(8,128)(2,1)} %bitcast.154) | data formatting | bytes 67108864 | tf_op jit(solution)/shard_map/all_to_all | solution.py:73
  (529 shorter events, 607.4 us)
Async XLA Ops:
  0.6 1099.5 %copy-start = (bf16[2048,128]{1,0:T(8,128)(2,1)S(1)}, bf16[2048,128]{1,0:T(8,128)(2,1)}, u32[]{:S(2)}) copy-start(bf16[2048,128]{1,0:T(8,128)(2,1)} %param.15) | copy-start | bytes 1572868
  7.3 9.2 copy-start.5
  7.3 61.4 %all-to-all-start.2 = ((bf16[2,256,32,128]{3,1,0,2:T(8,128)(2,1)}), bf16[2,256,32,128]{3,1,0,2:T(8,128)(2,1)}, u32[]{:S(2)}, u32[]{:S(2)}) async-start(bf16[2,256,32,128]{3,1,0,2:T(8,128)(2,1)} %bitcast.156), calls=%async_computation.2 | async-start | bytes 8388608 | tf_op jit(solution)/shard_map/all_to_all | solution.py:64
  71.8 7.9 copy-start.6
  71.8 60.0 %all-to-all-start.1 = ((bf16[2,256,32,128]{3,1,0,2:T(8,128)(2,1)}), bf16[2,256,32,128]{3,1,0,2:T(8,128)(2,1)}, u32[]{:S(2)}, u32[]{:S(2)}) async-start(bf16[2,256,32,128]{3,1,0,2:T(8,128)(2,1)} %bitcast.157), calls=%async_computation.1 | async-start | bytes 8388608 | tf_op jit(solution)/shard_map/all_to_all | solution.py:63
  131.8 63.1 %all-to-all-start = ((bf16[2,256,32,128]{3,1,0,2:T(8,128)(2,1)}), bf16[2,256,32,128]{3,1,0,2:T(8,128)(2,1)}, u32[]{:S(2)}, u32[]{:S(2)}) async-start(bf16[2,256,32,128]{3,1,0,2:T(8,128)(2,1)} %copy.43), calls=%async_computation | async-start | bytes 8388608 | tf_op jit(solution)/shard_map/all_to_all | solution.py:62
  207.6 2.2 copy-start.1
  220.3 2.2 copy-start.1
  233.1 2.2 copy-start.1
  245.9 2.2 copy-start.1
  258.6 2.2 copy-start.1
  271.4 2.2 copy-start.1
  284.2 2.2 copy-start.1
  296.9 2.2 copy-start.1
  309.7 2.2 copy-start.1
  322.5 2.2 copy-start.1
  335.2 2.2 copy-start.1
  348.0 2.2 copy-start.1
  360.8 2.2 copy-start.1
  373.5 2.2 copy-start.1
  399.1 2.2 copy-start.1
  411.8 2.2 copy-start.1
  462.9 2.2 copy-start.1
  475.7 2.2 copy-start.1
  514.0 2.2 copy-start.1
  526.7 2.2 copy-start.1
  539.5 2.2 copy-start.1
  577.8 2.2 copy-start.1
  590.6 2.2 copy-start.1
  641.6 2.2 copy-start.1
  654.4 2.2 copy-start.1
  705.5 2.2 copy-start.1
  718.2 2.2 copy-start.1
  756.5 2.2 copy-start.1
  769.3 2.2 copy-start.1
  782.1 2.2 copy-start.1
  820.4 2.2 copy-start.1
  833.1 2.2 copy-start.1
  884.2 2.2 copy-start.1
  897.0 2.2 copy-start.1
  948.0 2.2 copy-start.1
  960.8 2.2 copy-start.1
  999.1 2.2 copy-start.1
  1026.7 6.3 copy-start.4
  1026.7 58.9 %all-to-all-start.3 = ((bf16[2,8192,1,128]{3,0,2,1:T(2,128)(2,1)}), bf16[2,8192,1,128]{3,0,2,1:T(2,128)(2,1)}, u32[]{:S(2)}, u32[]{:S(2)}) async-start(bf16[2,8192,1,128]{3,0,2,1:T(2,128)(2,1)} %copy.52), calls=%async_computation.3 | async-start | bytes 8388608 | tf_op jit(solution)/shard_map/all_to_all | solution.py:69
  1085.7 2.9 copy-start.7
  1100.1 21.9 %copy-start.3 = (bf16[2,256,2048]{2,1,0:T(8,128)(2,1)}, bf16[2,256,2048]{2,1,0:T(8,128)(2,1)S(1)}, u32[]{:S(2)}) copy-start(bf16[2,256,2048]{2,1,0:T(8,128)(2,1)S(1)} %fusion.33) | copy-start | bytes 6291460
  1100.2 5.2 copy-start.2
  (27 other events, 59.3 us)
where the time goes:
time: 1600 us; the launch traced here: 1580 us
  matrix products  494 us (31%)
  blocking collectives  401 us (25%)
  local copies, waits for them, and re-layouts  183 us (11%)
  waiting for transfers between devices  175 us (11%)
  other arithmetic  172 us (11%)
  loops' own time  118 us (7%)
  starting transfers between devices  32 us (2%)
    all_to_all x1, blocking collectives, local_step(): recv_rows = lax.all_to_all(send_rows, 'sp', 1, 2, tiled=True)  401 us
    dot_general x64, matrix products, one_block(): jnp.einsum('mqhgd,mkhd->mhgqk', q_blk, key_rows, preferred_element_type=j...  273 us
    dot_general x64, matrix products, one_block(): jnp.einsum('mhgqk,mkhd->mqhgd', attn_probs, value_rows, preferred_element...  165 us
    another operation x1, loops' own time, causal_attention(): blocks = lax.map(one_block, jnp.arange(q_len // q_block) * q_block)  118 us
    reduce_sum x64, other arithmetic, one_block(): attn_probs = jax.nn.softmax(scores, axis=-1).astype(jnp.bfloat16)  86.4 us
    while x128, local copies, waits for them, and re-layouts  53.6 us
    all_to_all x1, waiting for transfers between devices, local_step(): value_rows = lax.all_to_all(value_rows, 'sp', 2, 1, tiled=True)  49.4 us
    all_to_all x1, waiting for transfers between devices, local_step(): queries = lax.all_to_all(queries, 'sp', 2, 1, tiled=True)  45.1 us
  transfers between devices with their start and end apart: 4, of which 4 were waited for; matrix products, arithmetic and copies ran while one was open for 2% of the time, Pallas kernels for 0%

commit v1 on v0

v1 whole, which is shorter than its diff:
```python
import functools
import math
import jax
import jax.numpy as jnp
from jax import lax
from jax.experimental import pallas as pl
from jax.experimental.pallas import tpu as pltpu
from jax.sharding import PartitionSpec as P

F32 = jnp.float32
BF16 = jnp.bfloat16
ANY = pl.BlockSpec(memory_space=pl.ANY)


def attention_kernel(first, q_block, per_step, blk, q_ref, kv_ref, *rest):
    o_ref, m_ref, l_ref, acc_ref = rest[-4:]
    i = pl.program_id(0) + first
    ring = kv_ref.shape[0]
    hd = q_ref.shape[1]
    step_keys = per_step * blk
    scale = math.log2(math.e) / math.sqrt(hd)
    m_ref[...] = jnp.full(m_ref.shape, -jnp.inf, F32)
    l_ref[...] = jnp.zeros(l_ref.shape, F32)
    acc_ref[...] = jnp.zeros(acc_ref.shape, F32)

    def step(j, masked):
        keys, values = [], []
        for u in range(per_step):
            b = j * per_step + u
            keys.append(kv_ref[lax.rem(b, ring), lax.div(b, ring), :, :hd])
            values.append(kv_ref[lax.rem(b, ring), lax.div(b, ring), :, hd:])
        k = jnp.concatenate(keys, axis=0)
        v = jnp.concatenate(values, axis=0)
        s = lax.dot_general(q_ref[...], k, (((1,), (1,)), ((), ())), preferred_element_type=F32)
        if masked:
            row = lax.broadcasted_iota(jnp.int32, s.shape, 0)
            col = lax.broadcasted_iota(jnp.int32, s.shape, 1)
            s = jnp.where(row >= col, s, -jnp.inf)
        top = s[:, :hd]
        for u in range(1, step_keys // hd):
            top = jnp.maximum(top, s[:, u * hd:(u + 1) * hd])
        m_old = m_ref[...]
        m_new = jnp.maximum(m_old, jnp.max(top, axis=1, keepdims=True))
        m_ref[...] = m_new
        alpha = jnp.exp2((m_old - m_new) * scale)
        m_scaled = m_new * scale
        parts = [jnp.exp2(s[:, u * hd:(u + 1) * hd] * scale - m_scaled) for u in range(step_keys // hd)]
        total = parts[0]
        for part in parts[1:]:
            total = total + part
        l_ref[...] = l_ref[...] * alpha + total
        p = jnp.concatenate([part.astype(BF16) for part in parts], axis=1)
        acc_ref[...] = acc_ref[...] * alpha + jnp.dot(p, v, preferred_element_type=F32)

    lax.fori_loop(0, i, lambda j, c: (step(j, False), c)[1], 0)
    step(i, True)
    o_ref[...] = (acc_ref[...] / jnp.sum(l_ref[...], axis=1, keepdims=True)).astype(BF16)


def attention(q, kv, lo, hi, q_block, into=None, after=()):
    seq, hd = q.shape
    ring, rows, blk, _ = kv.shape
    steps = hi - lo
    extra = list(after) + ([into] if into is not None else [])
    frac = (hi * hi - lo * lo) * q_block * q_block / 2
    return pl.pallas_call(
        functools.partial(attention_kernel, lo, q_block, q_block // blk, blk),
        grid=(steps,),
        in_specs=[
            pl.BlockSpec((q_block, hd), lambda i: (i + lo, 0)),
            pl.BlockSpec((ring, rows, blk, 2 * hd), lambda i: (0, 0, 0, 0)),
        ] + [ANY] * len(extra),
        out_specs=pl.BlockSpec((q_block, hd), lambda i: (i + lo, 0)),
        out_shape=jax.ShapeDtypeStruct((seq, hd), BF16),
        scratch_shapes=[pltpu.VMEM((q_block, hd), F32)] * 3,
        input_output_aliases={1 + len(extra): 0} if into is not None else {},
        cost_estimate=pl.CostEstimate(flops=int(16 * hd * frac), bytes_accessed=int(seq * hd * 8), transcendentals=int(frac)),
        name='attend',
    )(q, kv, *extra)


def project_kernel(heads_blk, pair, o_ref, w_ref, x_ref, ids_ref, wr_ref, *rest):
    h_ref, g_ref, acc_ref = rest[-3:]
    step = pl.program_id(0)

    @pl.when(step == 0)
    def _():
        acc_ref[...] = jnp.zeros(acc_ref.shape, F32)

    o = jnp.concatenate([o_ref[u] for u in range(heads_blk)], axis=1)
    w = w_ref[...].reshape(heads_blk * w_ref.shape[1], w_ref.shape[2])
    acc_ref[...] += jnp.dot(o, w, preferred_element_type=F32)

    @pl.when(step == pl.num_programs(0) - 1)
    def _():
        h = (x_ref[...].astype(F32) + acc_ref[...]).astype(BF16)
        h_ref[...] = h
        logits = jnp.dot(h, wr_ref[...], preferred_element_type=F32)
        expert = lax.broadcasted_iota(jnp.int32, logits.shape, 1)
        chosen = ids_ref[:, 0:1] == expert
        for u in range(1, ids_ref.shape[1]):
            chosen = jnp.logical_or(chosen, ids_ref[:, u:u + 1] == expert)
        picked = jnp.where(chosen, logits, -jnp.inf)
        e = jnp.exp(picked - jnp.max(picked, axis=1, keepdims=True))
        g_ref[...] = (e / jnp.sum(e, axis=1, keepdims=True)).T


def project(o, w_out, x, ids, w_router, after=()):
    heads, tok, hd = o.shape
    width = w_out.shape[2]
    experts = w_router.shape[1]
    heads_blk = min(heads, 8)
    return pl.pallas_call(
        functools.partial(project_kernel, heads_blk, 2),
        grid=(heads // heads_blk,),
        in_specs=[
            pl.BlockSpec((heads_blk, tok, hd), lambda i: (i, 0, 0)),
            pl.BlockSpec((heads_blk, hd, width), lambda i: (i, 0, 0)),
            pl.BlockSpec((tok, width), lambda i: (0, 0)),
            pl.BlockSpec((tok, ids.shape[1]), lambda i: (0, 0)),
            pl.BlockSpec((width, experts), lambda i: (0, 0)),
        ] + [ANY] * len(after),
        out_specs=[
            pl.BlockSpec((tok, width), lambda i: (0, 0)),
            pl.BlockSpec((experts, tok), lambda i: (0, 0)),
        ],
        out_shape=[jax.ShapeDtypeStruct((tok, width), BF16), jax.ShapeDtypeStruct((experts, tok), F32)],
        scratch_shapes=[pltpu.VMEM((tok, width), F32)],
        cost_estimate=pl.CostEstimate(flops=2 * tok * heads * hd * width, bytes_accessed=heads * hd * width * 2, transcendentals=0),
        name='project',
    )(o, w_out, x, ids, w_router, *after)


def rows_kernel(h_ref, rank_ref, gate_ref, *rest):
    out_ref = rest[-1]
    experts, cap = out_ref.shape[1], out_ref.shape[2]
    tok = h_ref.shape[0]
    slot = lax.broadcasted_iota(jnp.int32, (cap, tok), 0).astype(F32)
    hot, gate = [], []
    for e in range(experts):
        here = rank_ref[0, 0, e:e + 1, :] == slot
        hot.append(jnp.where(here, 1.0, 0.0))
        gate.append(jnp.sum(jnp.where(here, gate_ref[0, e:e + 1, :], 0.0), axis=1, keepdims=True))
    select = jnp.concatenate(hot, axis=0).astype(BF16)
    gates = jnp.concatenate(gate, axis=0)
    rows = jnp.dot(select, h_ref[...], preferred_element_type=F32)
    out_ref[0] = (rows * gates).astype(BF16).reshape(experts, cap, h_ref.shape[1])


def expert_rows(h_all, ranks, gates, micro, cap, into=None, after=()):
    sources, n_micro, experts, tok = ranks.shape
    width = h_all.shape[1]
    extra = list(after) + ([into] if into is not None else [])
    return pl.pallas_call(
        rows_kernel,
        grid=(sources,),
        in_specs=[
            pl.BlockSpec((tok, width), lambda s: (s, 0)),
            pl.BlockSpec((1, 1, experts, tok), lambda s: (s, micro, 0, 0)),
            pl.BlockSpec((1, experts, tok), lambda s: (s, 0, 0)),
        ] + [ANY] * len(extra),
        out_specs=pl.BlockSpec((1, experts, cap, width), lambda s: (micro, 0, s, 0)),
        out_shape=jax.ShapeDtypeStruct((n_micro, experts, sources * cap, width), BF16),
        input_output_aliases={2 + len(extra): 0} if into is not None else {},
        cost_estimate=pl.CostEstimate(flops=2 * sources * experts * cap * tok * width, bytes_accessed=2 * sources * (tok + experts * cap) * width, transcendentals=0),
        name='expert_rows',
    )(h_all, ranks, gates, *extra)


def slot_ranks(ids, experts, cap):
    tok = ids.shape[1]
    hot = jnp.any(ids[:, None, :, :] == jnp.arange(experts)[None, :, None, None], axis=-1)
    earlier = (jnp.arange(tok)[:, None] < jnp.arange(tok)[None, :]).astype(BF16)
    rank = jnp.einsum('met,ts->mes', hot.astype(BF16), earlier, preferred_element_type=F32)
    return jnp.where(jnp.logical_and(hot, rank < cap), rank, -1.0)


def solution(mesh):
    groups = mesh.shape['sp']

    def local_step(tokens, expert_ids, w_query, w_key, w_value, w_out, w_router):
        n_micro, tok, width = tokens.shape
        top_k = expert_ids.shape[2]
        heads, hd = w_query.shape[1:]
        kv_heads = w_key.shape[1]
        experts = w_router.shape[1]
        own = experts // groups
        cap = 2 * tok * top_k // experts
        share = groups // kv_heads
        seq = groups * tok
        columns = [[r + share * y for y in range(kv_heads)] for r in range(share)]
        rows = [[r + share * y for r in range(share)] for y in range(kv_heads)]
        q_block = min(2 * tok, seq)
        n_blk = seq // q_block

        def swap(a, **kw):
            return lax.all_to_all(a, 'sp', 0, 0, tiled=True, **kw)

        w_kv = jnp.concatenate([w_key, w_value], axis=2)
        kv = jnp.einsum('mtd,dhk->mhtk', tokens, w_kv, preferred_element_type=F32).astype(BF16)
        kv_held = []
        for m in range(n_micro):
            mine = swap(kv[m], axis_index_groups=columns)
            gathered = lax.all_gather(mine, 'sp', axis=0, axis_index_groups=rows)
            kv_held.append(gathered.reshape(share, kv_heads, tok, 2 * hd))
        ranks = slot_ranks(expert_ids, experts, cap).reshape(n_micro, groups, own, tok)
        ranks = swap(ranks.transpose(1, 0, 2, 3))
        q = jnp.einsum('mtd,dhk->mhtk', tokens, w_query, preferred_element_type=F32).astype(BF16)
        q_held = [swap(q[m]).reshape(seq, hd) for m in range(n_micro)]

        hidden, buffers, gathered = [], None, []
        attn = attention(q_held[0], kv_held[0], 0, n_blk, q_block)
        for m in range(n_micro):
            o = swap(attn.reshape(groups, tok, hd))
            part = None
            if m + 1 < n_micro:
                cut = (5 * n_blk) // 8
                part = attention(q_held[m + 1], kv_held[m + 1], 0, cut, q_block)
            h, gate = project(o, w_out, tokens[m], expert_ids[m], w_router, after=() if part is None else (part,))
            hidden.append(h)
            h_all = lax.all_gather(h, 'sp', axis=0, tiled=True)
            gates = swap(gate.reshape(groups, own, tok))
            gathered.append((h_all, gates))
            if part is not None:
                attn = attention(q_held[m + 1], kv_held[m + 1], cut, n_blk, q_block, into=part, after=(h,))
        for m in range(n_micro):
            h_all, gates = gathered[m]
            buffers = expert_rows(h_all, ranks, gates, m, cap, into=buffers, after=(attn,) if m == 0 else ())
        return jnp.stack(hidden), buffers

    return jax.shard_map(
        local_step,
        mesh=mesh,
        in_specs=(P('dp', 'sp', None), P('dp', 'sp', None), P(), P(), P(), P(), P()),
        out_specs=(P('dp', 'sp', None), P('dp', 'sp', None, None)),
        check_vma=False,
    )
```

time: 1600 us -> 564 us (0.35); the launches traced: 1580 us -> 562 us
  matrix products: 494 us -> 19.5 us
  blocking collectives: 401 us -> 52.8 us
  Pallas kernels: 0 us -> 259 us
  other arithmetic: 172 us -> 2.32 us
  local copies, waits for them, and re-layouts: 183 us -> 28.9 us
  loops' own time: 118 us -> 0 us
  waiting for transfers between devices: 175 us -> 147 us
    dot_general x136 -> x3, matrix products: 494 us -> 19.5 us  [the longest x1 14.1 us: local_step(): jnp.einsum('mtd,dhk->mhtk', tokens, w_query, preferred_element_type=F32)]
    all_to_all x1 -> x2, blocking collectives: 401 us -> 52.8 us  [swap(): return lax.all_to_all(a, 'sp', 0, 0, tiled=True, **kw)]
    pallas_call x0 -> x7, Pallas kernels: none -> 259 us  [the longest x3 176 us: attention(): pl.pallas_call(functools.partial(attention_kernel, lo, q_block, q_block /...]
    another operation x1 -> x0, loops' own time: 118 us -> none  [causal_attention(): blocks = lax.map(one_block, jnp.arange(q_len // q_block) * q_block)]
    all_to_all x4 -> x7, waiting for transfers between devices: 175 us -> 83.8 us  [swap(): return lax.all_to_all(a, 'sp', 0, 0, tiled=True, **kw)]
    reduce_sum x66 -> x0, other arithmetic: 89.2 us -> none  [the longest x64 86.4 us: one_block(): attn_probs = jax.nn.softmax(scores, axis=-1).astype(jnp.bfloat16)]
    all_gather x0 -> x4, waiting for transfers between devices: none -> 63 us  [the longest x2 63 us: local_step(): h_all = lax.all_gather(h, 'sp', axis=0, tiled=True)]
    while x128 -> x0, local copies, waits for them, and re-layouts: 53.6 us -> none
  transfers between devices with their start and end apart: 4 -> 11, of which waited for: 4 -> 5; matrix products, arithmetic and copies ran while one was open for 2% -> 6% of each run, Pallas kernels for 0% -> 39%
where the time goes in v1:
time: 564 us; the launch traced here: 562 us
  Pallas kernels  259 us (46%)
  waiting for transfers between devices  147 us (26%)
  blocking collectives  52.8 us (9%)
  starting transfers between devices  37.6 us (7%)
  local copies, waits for them, and re-layouts  28.9 us (5%)
  matrix products  19.5 us (3%)
  between operations  14 us (2%)
    pallas_call x3, Pallas kernels, attention(): pl.pallas_call(functools.partial(attention_kernel, lo, q_block, q_block /...  176 us
    all_to_all x7, waiting for transfers between devices, swap(): return lax.all_to_all(a, 'sp', 0, 0, tiled=True, **kw)  83.8 us
    all_gather x2, waiting for transfers between devices, local_step(): h_all = lax.all_gather(h, 'sp', axis=0, tiled=True)  63 us
    pallas_call x2, Pallas kernels, expert_rows(): pl.pallas_call(rows_kernel, grid=(sources,), in_specs=[pl.BlockSpec((tok,...  61.6 us
    all_to_all x2, blocking collectives, swap(): return lax.all_to_all(a, 'sp', 0, 0, tiled=True, **kw)  52.8 us
    all_to_all x7, starting transfers between devices, swap(): return lax.all_to_all(a, 'sp', 0, 0, tiled=True, **kw)  37.1 us
    pallas_call x2, Pallas kernels, project(): pl.pallas_call(functools.partial(project_kernel, heads_blk, 2), grid=(hea...  22.3 us
    dot_general x1, matrix products, local_step(): jnp.einsum('mtd,dhk->mhtk', tokens, w_query, preferred_element_type=F32)  14.1 us
  transfers between devices with their start and end apart: 11, of which 5 were waited for; matrix products, arithmetic and copies ran while one was open for 6% of the time, Pallas kernels for 39%

profile of v1, /device:TPU:97, one launch (start us, length us, event | category | flops | bytes accessed | tf_op | source)
XLA Modules:
  0.0 561.6 jit_solution(6438003354011146554)
XLA Ops:
  7.2 0.1 all-gather.11.cloned.1.call-start
  7.3 4.4 copy.47
  11.6 2.6 copy.48
  14.2 5.2 fusion.13
  19.4 0.9 slice_bitcast_fusion.5
  20.3 15.0 %all_to_all.45 = bf16[4,256,256]{1,2,0:T(8,128)(2,1)S(1)} all-to-all(bf16[4,256,256]{1,2,0:T(8,128)(2,1)S(1)} %get-tuple-element.14), channel_id=1, replica_groups={{0,8,16,24},{1,9,17,25},{2,10,18,26},{3,11,19,27},{4,12,20,28},{5,13,21..., dimensions={0} | all-to-all | bytes 1048576 | tf_op jit(solution)/shard_map/all_to_all | solution.py:197
  35.3 1.0 copy.49
  36.4 3.6 all-to-all-start.4
  39.9 14.1 %convert_bitcast_fusion = bf16[2,32,256,128]{2,3,0,1:T(8,128)(2,1)S(1)} fusion(bf16[2048,32,128,1]{2,1,0,3:T(8,128)(2,1)} %bitcast.65, bf16[2,256,2048]{2,1,0:T(8,128)(2,1)S(1)} %copy-done.6), kind=kOutput, calls=%fused_computation.6 | convolution fusion | flops 8592031744 | bytes 23068672 | tf_op jit(solution)/shard_map/mtd,dhk->mhtk/dot_general | solution.py:208
  54.1 1.7 slice_bitcast_fusion.1
  55.8 37.8 %all_to_all.46 = bf16[32,256,128]{1,2,0:T(8,128)(2,1)} all-to-all(bf16[32,256,128]{1,2,0:T(8,128)(2,1)S(1)} %get-tuple-element.11), channel_id=1, replica_groups=mesh['dp'=1,'sp'=32] {'sp'}, dimensions={0} | all-to-all | bytes 4194304 | tf_op jit(solution)/shard_map/all_to_all | solution.py:197
  93.6 3.2 all-to-all-start
  96.8 0.2 all-gather.13.cloned.1.call-start
  97.0 1.1 copy.52
  98.2 0.6 fusion.22
  98.8 0.8 copy.60
  99.5 3.2 slice_bitcast_fusion.2
  102.7 4.1 copy.51
  106.8 24.1 %all-to-all-done = bf16[32,256,128]{1,2,0:T(8,128)(2,1)S(1)} async-done(((bf16[32,256,128]{1,2,0:T(8,128)(2,1)}), bf16[32,256,128]{1,2,0:T(8,128)(2,1)S(1)}, u32[]{:S(2)}, u32[]{:S(2)}) %all-to-all-start) | async-done | bytes 2097184 | tf_op jit(solution)/shard_map/all_to_all | solution.py:197
  130.9 2.8 copy.46
  133.7 86.3 %attend.3 = bf16[8192,128]{1,0:T(8,128)(2,1)} custom-call(bf16[8192,128]{1,0:T(8,128)(2,1)} %bitcast.61, bf16[8,4,256,256]{3,2,1,0:T(8,128)(2,1)} %bitcast.66), custom_call_target="tpu_custom_call" | custom-call | flops 68719476736 | bytes 8388608 | tf_op jit(solution)/shard_map/attend/pallas_call | solution.py:66
  220.0 11.2 %all-to-all-start.2 = ((bf16[32,256,128]{2,1,0:T(8,128)(2,1)}), bf16[32,256,128]{2,1,0:T(8,128)(2,1)S(1)}, u32[]{:S(2)}, u32[]{:S(2)}) async-start(bf16[32,256,128]{2,1,0:T(8,128)(2,1)} %bitcast.60), calls=%async_computation.2 | async-start | bytes 4194304 | tf_op jit(solution)/shard_map/all_to_all | solution.py:197
  231.3 0.1 all-gather.9.cloned.1.call-start
  231.4 36.9 %attend.4.rest_0_.rest_1_ = bf16[8192,128]{1,0:T(8,128)(2,1)} custom-call(bf16[8192,128]{1,0:T(8,128)(2,1)} %bitcast.58, bf16[8,4,256,256]{3,2,1,0:T(8,128)(2,1)} %bitcast.67), custom_call_target="tpu_custom_call" | custom-call | flops 26843545600 | bytes 8388608 | tf_op jit(solution)/shard_map/attend/pallas_call | solution.py:66
  268.2 1.3 copy-done.1
  269.6 11.2 %project.2 = (bf16[256,2048]{1,0:T(8,128)(2,1)}, f32[128,256]{1,0:T(8,128)}) custom-call(bf16[32,256,128]{2,1,0:T(8,128)(2,1)} %copy-done.1, bf16[32,128,2048]{2,1,0:T(8,128)(2,1)} %w_ref.3, bf16[256,2048]{1,0:T(8,128)(2,1)} %get-tuple-element.13.x_ref, s32[256,8]{1,0:T(8,128)} %bitcast.63, bf16[2048,128]{1,0:T(8,128)(2,1)} %wr_ref.3, ...), custom_call_target="tpu_custom_call" | custom-call | flops 4294967296 | bytes 16777216 | tf_op jit(solution)/shard_map/project/pallas_call | solution.py:113
  280.8 52.4 %attend.5.rest_0_ = bf16[8192,128]{1,0:T(8,128)(2,1)} custom-call(bf16[8192,128]{1,0:T(8,128)(2,1)} %bitcast.59, bf16[8,4,256,256]{3,2,1,0:T(8,128)(2,1)} %bitcast.68, bf16[256,2048]{1,0:T(8,128)(2,1)} %get-tuple-element.6.rest_0_, bf16[8192,128]{1,0:T(8,128)(2,1)} %attend.4.rest_0_.rest_1_), custom_call_target="tpu_custom_call", output_to_operand_aliasing={{}: (3, {})} | custom-call | flops 41875931136 | bytes 8388608 | tf_op jit(solution)/shard_map/attend/pallas_call | solution.py:66
  333.2 6.7 %all-to-all-start.5 = ((bf16[32,256,128]{2,1,0:T(8,128)(2,1)}), bf16[32,256,128]{2,1,0:T(8,128)(2,1)S(1)}, u32[]{:S(2)}, u32[]{:S(2)}) async-start(bf16[32,256,128]{2,1,0:T(8,128)(2,1)} %bitcast.55), calls=%async_computation.5 | async-start | bytes 4194304 | tf_op jit(solution)/shard_map/all_to_all | solution.py:197
  339.9 0.1 all-gather.7.cloned.1.call-start
  340.0 0.8 copy.61
  340.8 46.2 %all-to-all-done.5.o_ref = bf16[32,256,128]{2,1,0:T(8,128)(2,1)S(1)} async-done(((bf16[32,256,128]{2,1,0:T(8,128)(2,1)}), bf16[32,256,128]{2,1,0:T(8,128)(2,1)S(1)}, u32[]{:S(2)}, u32[]{:S(2)}) %all-to-all-start.5) | async-done | bytes 2097184 | tf_op jit(solution)/shard_map/all_to_all | solution.py:197
  387.0 1.3 copy-done
  388.3 11.2 %project.3 = (bf16[256,2048]{1,0:T(8,128)(2,1)}, f32[128,256]{1,0:T(8,128)}) custom-call(bf16[32,256,128]{2,1,0:T(8,128)(2,1)} %copy-done, bf16[32,128,2048]{2,1,0:T(8,128)(2,1)} %w_ref.3, bf16[256,2048]{1,0:T(8,128)(2,1)} %get-tuple-element.12.x_ref, s32[256,8]{1,0:T(8,128)} %bitcast.64, bf16[2048,128]{1,0:T(8,128)(2,1)} %wr_ref.3), custom_call_target="tpu_custom_call" | custom-call | flops 4294967296 | bytes 16777216 | tf_op jit(solution)/shard_map/project/pallas_call | solution.py:113
  399.5 0.8 fusion.9
  400.4 0.2 and_select_fusion
  400.6 0.2 copy.54
  400.8 0.8 copy.67
  401.6 6.7 %all-to-all-start.6 = ((f32[32,2,4,256]{3,2,1,0:T(4,128)}), f32[32,2,4,256]{3,2,1,0:T(4,128)S(1)}, u32[]{:S(2)}, u32[]{:S(2)}) async-start(f32[32,2,4,256]{3,2,1,0:T(4,128)} %bitcast.54), calls=%async_computation.6 | async-start | bytes 524288 | tf_op jit(solution)/shard_map/all_to_all | solution.py:197
  408.3 0.7 reshape.32
  409.0 8.2 %all-to-all-done.6.rank_ref = f32[32,2,4,256]{3,2,1,0:T(4,128)S(1)} async-done(((f32[32,2,4,256]{3,2,1,0:T(4,128)}), f32[32,2,4,256]{3,2,1,0:T(4,128)S(1)}, u32[]{:S(2)}, u32[]{:S(2)}) %all-to-all-start.6) | async-done | bytes 262176 | tf_op jit(solution)/shard_map/all_to_all | solution.py:197
  417.2 2.9 all-to-all-start.8
  420.1 1.5 pad_maximum_fusion
  421.6 0.7 reshape.31
  422.3 5.3 all-to-all-done.8.gate_ref
  427.6 2.9 all-to-all-start.7
  430.5 30.8 %expert_rows.2.rest_0_ = bf16[2,4,1024,2048]{3,2,1,0:T(8,128)(2,1)} custom-call(bf16[8192,2048]{1,0:T(8,128)(2,1)} %all-gather.9.cloned.1.call-done.h_ref, f32[32,2,4,256]{3,2,1,0:T(4,128)} %copy-done.4, f32[32,4,256]{2,1,0:T(4,128)} %copy-done.7, bf16[8192,128]{1,0:T(8,128)(2,1)} %attend.5.rest_0_), custom_call_target="tpu_custom_call" | custom-call | flops 4294967296 | bytes 50331648 | tf_op jit(solution)/shard_map/expert_rows/pallas_call | solution.py:154
  461.3 62.9 %all-gather.7.cloned.1.call-done.h_ref = bf16[8192,2048]{1,0:T(8,128)(2,1)} async-done(((bf16[256,2048]{1,0:T(8,128)(2,1)}), bf16[8192,2048]{1,0:T(8,128)(2,1)}) %all-gather.7.cloned.1.call-update) | async-done | bytes 33554448 | tf_op jit(solution)/shard_map/all_gather | solution.py:221
  524.2 30.8 %expert_rows.3 = bf16[2,4,1024,2048]{3,2,1,0:T(8,128)(2,1)} custom-call(bf16[8192,2048]{1,0:T(8,128)(2,1)} %all-gather.7.cloned.1.call-done.h_ref, f32[32,2,4,256]{3,2,1,0:T(4,128)} %copy-done.4, f32[32,4,256]{2,1,0:T(4,128)} %copy-done.8, bf16[2,4,1024,2048]{3,2,1,0:T(8,128)(2,1)} %expert_rows.2.rest_0_), custom_call_target="tpu_custom_call", output_to_operand_aliasing={{}: (3, {})} | custom-call | flops 4294967296 | bytes 50331648 | tf_op jit(solution)/shard_map/expert_rows/pallas_call | solution.py:154
  (36 shorter events, 0.3 us)
Async XLA Ops:
  7.2 4.5 copy-start.5
  7.2 126.6 %all-gather.11.cloned.1.call-start = ((), (), s32[]{:S(2)}) async-start(), calls=%async_computation.11 | async-start | bytes 4718592 | tf_op jit(solution)/shard_map/all_gather | solution.py:204
  20.3 19.6 %copy-start.6 = (bf16[2,256,2048]{2,1,0:T(8,128)(2,1)S(1)}, bf16[2,256,2048]{2,1,0:T(8,128)(2,1)}, u32[]{:S(2)}) copy-start(bf16[2,256,2048]{2,1,0:T(8,128)(2,1)} %param.7) | copy-start | bytes 6291460
  36.4 19.4 %all-to-all-start.4 = ((bf16[4,256,256]{1,2,0:T(8,128)(2,1)}), bf16[4,256,256]{1,2,0:T(8,128)(2,1)S(1)}, u32[]{:S(2)}, u32[]{:S(2)}) async-start(bf16[4,256,256]{1,2,0:T(8,128)(2,1)} %get-tuple-element.15), calls=%async_computation.4 | async-start | bytes 1048576 | tf_op jit(solution)/shard_map/all_to_all | solution.py:197
  93.6 4.6 copy-start.11
  93.6 37.3 %all-to-all-start = ((bf16[32,256,128]{1,2,0:T(8,128)(2,1)}), bf16[32,256,128]{1,2,0:T(8,128)(2,1)S(1)}, u32[]{:S(2)}, u32[]{:S(2)}) async-start(bf16[32,256,128]{1,2,0:T(8,128)(2,1)} %get-tuple-element.10), calls=%async_computation | async-start | bytes 4194304 | tf_op jit(solution)/shard_map/all_to_all | solution.py:197
  96.8 134.6 %all-gather.13.cloned.1.call-start = ((), (), s32[]{:S(2)}) async-start(), calls=%async_computation.12 | async-start | bytes 4718592 | tf_op jit(solution)/shard_map/all_gather | solution.py:204
  220.0 48.2 %all-to-all-start.2 = ((bf16[32,256,128]{2,1,0:T(8,128)(2,1)}), bf16[32,256,128]{2,1,0:T(8,128)(2,1)S(1)}, u32[]{:S(2)}, u32[]{:S(2)}) async-start(bf16[32,256,128]{2,1,0:T(8,128)(2,1)} %bitcast.60), calls=%async_computation.2 | async-start | bytes 4194304 | tf_op jit(solution)/shard_map/all_to_all | solution.py:197
  231.3 199.2 %all-gather.9.cloned.1.call-start = ((), (), s32[]{:S(2)}) async-start(), calls=%async_computation.10 | async-start | bytes 34603008 | tf_op jit(solution)/shard_map/all_gather | solution.py:221
  268.2 1.3 copy-start.1
  333.2 6.8 %copy-start.13 = (s32[1,256,8]{1,2,0:T(8,128)S(1)}, s32[1,256,8]{1,2,0:T(8,128)}, u32[]{:S(2)}) copy-start(s32[1,256,8]{1,2,0:T(8,128)} %get-tuple-element.16) | copy-start | bytes 24580
  333.2 53.8 %all-to-all-start.5 = ((bf16[32,256,128]{2,1,0:T(8,128)(2,1)}), bf16[32,256,128]{2,1,0:T(8,128)(2,1)S(1)}, u32[]{:S(2)}, u32[]{:S(2)}) async-start(bf16[32,256,128]{2,1,0:T(8,128)(2,1)} %bitcast.55), calls=%async_computation.5 | async-start | bytes 4194304 | tf_op jit(solution)/shard_map/all_to_all | solution.py:197
  339.9 184.3 %all-gather.7.cloned.1.call-start = ((), (), s32[]{:S(2)}) async-start(), calls=%async_computation.9 | async-start | bytes 34603008 | tf_op jit(solution)/shard_map/all_gather | solution.py:221
  387.0 1.3 copy-start
  388.3 11.3 %copy-start.12 = (s32[2,256,8]{1,2,0:T(8,128)S(1)}, s32[2,256,8]{1,2,0:T(8,128)}, u32[]{:S(2)}) copy-start(s32[2,256,8]{1,2,0:T(8,128)} %param.8) | copy-start | bytes 49156
  399.5 8.8 %copy-start.9 = (f32[128,256]{1,0:T(8,128)S(1)}, f32[128,256]{1,0:T(8,128)}, u32[]{:S(2)}) copy-start(f32[128,256]{1,0:T(8,128)} %get-tuple-element.9) | copy-start | bytes 393220
  399.5 20.6 %copy-start.2 = (bf16[256,2048]{1,0:T(8,128)(2,1)S(1)}, bf16[256,2048]{1,0:T(8,128)(2,1)}, u32[]{:S(2)}) copy-start(bf16[256,2048]{1,0:T(8,128)(2,1)} %get-tuple-element.6.rest_0_) | copy-start | bytes 3145732
  399.5 20.6 %copy-start.3 = (bf16[256,2048]{1,0:T(8,128)(2,1)S(1)}, bf16[256,2048]{1,0:T(8,128)(2,1)}, u32[]{:S(2)}) copy-start(bf16[256,2048]{1,0:T(8,128)(2,1)} %get-tuple-element.7) | copy-start | bytes 3145732
  401.6 15.6 %all-to-all-start.6 = ((f32[32,2,4,256]{3,2,1,0:T(4,128)}), f32[32,2,4,256]{3,2,1,0:T(4,128)S(1)}, u32[]{:S(2)}, u32[]{:S(2)}) async-start(f32[32,2,4,256]{3,2,1,0:T(4,128)} %bitcast.54), calls=%async_computation.6 | async-start | bytes 524288 | tf_op jit(solution)/shard_map/all_to_all | solution.py:197
  417.2 4.4 copy-start.4
  417.2 10.4 %all-to-all-start.8 = ((f32[32,4,256]{2,1,0:T(4,128)}), f32[32,4,256]{2,1,0:T(4,128)S(1)}, u32[]{:S(2)}, u32[]{:S(2)}) async-start(f32[32,4,256]{2,1,0:T(4,128)} %reshape.32), calls=%async_computation.8 | async-start | bytes 262144 | tf_op jit(solution)/shard_map/all_to_all | solution.py:197
  420.1 1.5 copy-start.10
  427.6 2.9 copy-start.7
  427.6 33.7 %all-to-all-start.7 = ((f32[32,4,256]{2,1,0:T(4,128)}), f32[32,4,256]{2,1,0:T(4,128)S(1)}, u32[]{:S(2)}, u32[]{:S(2)}) async-start(f32[32,4,256]{2,1,0:T(4,128)} %reshape.31), calls=%async_computation.7 | async-start | bytes 262144 | tf_op jit(solution)/shard_map/all_to_all | solution.py:197
  461.3 62.9 %copy-start.8 = (f32[32,4,256]{2,1,0:T(4,128)}, f32[32,4,256]{2,1,0:T(4,128)S(1)}, u32[]{:S(2)}) copy-start(f32[32,4,256]{2,1,0:T(4,128)S(1)} %all-to-all-done.7.gate_ref) | copy-start | bytes 393220
Sparse Core Ops, SparseCore 0:
  36.5 30.5 all-gather.10
  99.2 42.6 all-gather.12
  280.9 132.4 all-gather.8
  415.4 108.8 all-gather.6

commit v2 on v1

v2 whole, which is shorter than its diff:
```python
import functools
import math
import jax
import jax.numpy as jnp
from jax import lax
from jax.experimental import pallas as pl
from jax.experimental.pallas import tpu as pltpu
from jax.sharding import PartitionSpec as P

F32 = jnp.float32
BF16 = jnp.bfloat16
ANY = pl.BlockSpec(memory_space=pl.ANY)


def attention_kernel(first, q_ref, kv_ref, *rest):
    o_ref, q_rows, m_ref, l_ref, acc_ref = rest[-5:]
    i = pl.program_id(0) + first
    ring = kv_ref.shape[0]
    blk = kv_ref.shape[3]
    per_q, hd = q_ref.shape[0], q_ref.shape[1]
    scale = math.log2(math.e) / math.sqrt(hd)
    for u in range(per_q):
        q_rows[u * blk:(u + 1) * blk, :] = q_ref[u].T
    m_ref[...] = jnp.full(m_ref.shape, -jnp.inf, F32)
    l_ref[...] = jnp.zeros(l_ref.shape, F32)
    acc_ref[...] = jnp.zeros(acc_ref.shape, F32)

    half = q_rows.shape[0] // 2

    def step(start, count, spans, masked):
        keys, values = [], []
        for u in range(count):
            b = start + u
            keys.append(kv_ref[lax.rem(b, ring), lax.div(b, ring), :hd, :])
            values.append(kv_ref[lax.rem(b, ring), lax.div(b, ring), hd:, :])
        k = jnp.concatenate(keys, axis=1)
        v = jnp.concatenate(values, axis=1)
        scores = [jnp.dot(q_rows[span, :], k, preferred_element_type=F32) for span in spans]
        for span, s in zip(spans, scores):
            if masked:
                row = lax.broadcasted_iota(jnp.int32, s.shape, 0) + span.start
                col = lax.broadcasted_iota(jnp.int32, s.shape, 1)
                s = jnp.where(row >= col, s, -jnp.inf)
            pieces = [s[:, u:u + hd] for u in range(0, count * blk, hd)]
            m_old = m_ref[span, :]
            top = functools.reduce(jnp.maximum, pieces)
            m_new = jnp.maximum(m_old, jnp.max(top, axis=1, keepdims=True))
            m_ref[span, :] = m_new
            alpha = jnp.exp2((m_old - m_new) * scale)
            m_scaled = m_new * scale
            parts = [jnp.exp2(piece * scale - m_scaled) for piece in pieces]
            l_ref[span, :] = l_ref[span, :] * alpha + functools.reduce(jnp.add, parts)
            p = jnp.concatenate([part.astype(BF16) for part in parts], axis=1)
            o = lax.dot_general(p, v, (((1,), (1,)), ((), ())), preferred_element_type=F32)
            acc_ref[span, :] = acc_ref[span, :] * alpha + o

    def full(j, carry):
        step(j * per_q, per_q, [slice(0, half), slice(half, 2 * half)], False)
        return carry

    lax.fori_loop(0, i, full, 0)
    step(i * per_q, per_q, [slice(0, half), slice(half, 2 * half)], True)
    o_ref[...] = (acc_ref[...] / jnp.sum(l_ref[...], axis=1, keepdims=True)).astype(BF16)


def attention(q, kv, lo, hi, per_q, into=None, after=()):
    n_src, hd, blk = q.shape
    ring, rows = kv.shape[:2]
    q_block = per_q * blk
    seq = n_src * blk
    extra = list(after) + ([into] if into is not None else [])
    pairs = (hi * hi - lo * lo) * q_block * q_block / 2
    return pl.pallas_call(
        functools.partial(attention_kernel, lo),
        grid=(hi - lo,),
        in_specs=[
            pl.BlockSpec((per_q, hd, blk), lambda i: (i + lo, 0, 0)),
            pl.BlockSpec((ring, rows, 2 * hd, blk), lambda i: (0, 0, 0, 0)),
        ] + [ANY] * len(extra),
        out_specs=pl.BlockSpec((q_block, hd), lambda i: (i + lo, 0)),
        out_shape=jax.ShapeDtypeStruct((seq, hd), BF16),
        scratch_shapes=[pltpu.VMEM((q_block, hd), BF16)] + [pltpu.VMEM((q_block, hd), F32)] * 3,
        input_output_aliases={1 + len(extra): 0} if into is not None else {},
        cost_estimate=pl.CostEstimate(flops=int(4 * hd * pairs * 2), bytes_accessed=int(seq * hd * 8), transcendentals=int(pairs)),
        name='attend',
    )(q, kv, *extra)


def project_kernel(heads_blk, parts, o_ref, w_ref, x_ref, ids_ref, wr_ref, *rest):
    *part_refs, h_ref, g_ref, acc_ref = rest[-3 - parts:]
    step = pl.program_id(0)

    @pl.when(step == 0)
    def _():
        acc_ref[...] = jnp.zeros(acc_ref.shape, F32)

    o = jnp.concatenate([o_ref[u] for u in range(heads_blk)], axis=1)
    tile = min(w_ref.shape[2], 512)

    def add(c, carry):
        cols = pl.ds(pl.multiple_of(c * tile, tile), tile)
        w = w_ref[:, :, cols].reshape(heads_blk * w_ref.shape[1], tile)
        acc_ref[:, cols] += jnp.dot(o, w, preferred_element_type=F32)
        return carry

    lax.fori_loop(0, w_ref.shape[2] // tile, add, 0)

    @pl.when(step == pl.num_programs(0) - 1)
    def _():
        h = (x_ref[...].astype(F32) + acc_ref[...]).astype(BF16)
        h_ref[...] = h
        for u, part_ref in enumerate(part_refs):
            size = part_ref.shape[1]
            part_ref[...] = h[:, u * size:(u + 1) * size]
        logits = jnp.dot(h, wr_ref[...], preferred_element_type=F32)
        expert = lax.broadcasted_iota(jnp.int32, logits.shape, 1)
        chosen = ids_ref[:, 0:1] == expert
        for u in range(1, ids_ref.shape[1]):
            chosen = jnp.logical_or(chosen, ids_ref[:, u:u + 1] == expert)
        picked = jnp.where(chosen, logits, -jnp.inf)
        e = jnp.exp(picked - jnp.max(picked, axis=1, keepdims=True))
        g_ref[...] = (e / jnp.sum(e, axis=1, keepdims=True)).T


def project(o, w_out, x, ids, w_router, parts, after=()):
    heads, tok, hd = o.shape
    width = w_out.shape[2]
    experts = w_router.shape[1]
    heads_blk = min(heads, 8)
    return pl.pallas_call(
        functools.partial(project_kernel, heads_blk, parts),
        grid=(heads // heads_blk,),
        in_specs=[
            pl.BlockSpec((heads_blk, tok, hd), lambda i: (i, 0, 0)),
            pl.BlockSpec((heads_blk, hd, width), lambda i: (i, 0, 0)),
            pl.BlockSpec((tok, width), lambda i: (0, 0)),
            pl.BlockSpec((tok, ids.shape[1]), lambda i: (0, 0)),
            pl.BlockSpec((width, experts), lambda i: (0, 0)),
        ] + [ANY] * len(after),
        out_specs=[pl.BlockSpec((tok, width // parts), lambda i: (0, 0))] * parts + [
            pl.BlockSpec((tok, width), lambda i: (0, 0)),
            pl.BlockSpec((experts, tok), lambda i: (0, 0)),
        ],
        out_shape=[jax.ShapeDtypeStruct((tok, width // parts), BF16)] * parts + [
            jax.ShapeDtypeStruct((tok, width), BF16), jax.ShapeDtypeStruct((experts, tok), F32)],
        scratch_shapes=[pltpu.VMEM((tok, width), F32)],
        cost_estimate=pl.CostEstimate(flops=2 * tok * heads * hd * width, bytes_accessed=heads * hd * width * 2, transcendentals=0),
        name='project',
    )(o, w_out, x, ids, w_router, *after)


def rows_kernel(h_ref, rank_ref, gate_ref, *rest):
    out_ref = rest[-1]
    experts = out_ref.shape[1]
    some, _, tok = gate_ref.shape
    cap = out_ref.shape[2] // some
    slot = lax.broadcasted_iota(jnp.int32, (cap, tok), 0).astype(F32)

    def source(u, carry):
        hot, gate = [], []
        for e in range(experts):
            here = rank_ref[u, 0, e:e + 1, :] == slot
            hot.append(jnp.where(here, 1.0, 0.0))
            gate.append(jnp.sum(jnp.where(here, gate_ref[u, e:e + 1, :], 0.0), axis=1, keepdims=True))
        select = jnp.concatenate(hot, axis=0).astype(BF16)
        gates = jnp.concatenate(gate, axis=0)
        rows = jnp.dot(select, h_ref[pl.ds(pl.multiple_of(u * tok, tok), tok), :], preferred_element_type=F32)
        slots = pl.ds(pl.multiple_of(u * cap, cap), cap)
        out_ref[0, :, slots, :] = (rows * gates).astype(BF16).reshape(experts, cap, rows.shape[1])
        return carry

    lax.fori_loop(0, some, source, 0)


def expert_rows(h_all, ranks, gates, micro, cap, width, column, into=None, after=()):
    sources, n_micro, experts, tok = ranks.shape
    part = h_all.shape[1]
    some = min(sources, 4)
    extra = list(after) + ([into] if into is not None else [])
    return pl.pallas_call(
        rows_kernel,
        grid=(sources // some,),
        in_specs=[
            pl.BlockSpec((some * tok, part), lambda s: (s, 0)),
            pl.BlockSpec((some, 1, experts, tok), lambda s: (s, micro, 0, 0)),
            pl.BlockSpec((some, experts, tok), lambda s: (s, 0, 0)),
        ] + [ANY] * len(extra),
        out_specs=pl.BlockSpec((1, experts, some * cap, part), lambda s: (micro, 0, s, column)),
        out_shape=jax.ShapeDtypeStruct((n_micro, experts, sources * cap, width), BF16),
        input_output_aliases={2 + len(extra): 0} if into is not None else {},
        cost_estimate=pl.CostEstimate(flops=2 * sources * experts * cap * tok * part, bytes_accessed=2 * sources * (tok + experts * cap) * part, transcendentals=0),
        name='expert_rows',
    )(h_all, ranks, gates, *extra)


def slot_ranks(ids, experts, cap):
    tok = ids.shape[1]
    hot = jnp.any(ids[:, None, :, :] == jnp.arange(experts)[None, :, None, None], axis=-1)
    earlier = (jnp.arange(tok)[:, None] < jnp.arange(tok)[None, :]).astype(BF16)
    rank = jnp.einsum('met,ts->mes', hot.astype(BF16), earlier, preferred_element_type=F32)
    return jnp.where(jnp.logical_and(hot, rank < cap), rank, -1.0)


def solution(mesh):
    groups = mesh.shape['sp']

    def local_step(tokens, expert_ids, w_query, w_key, w_value, w_out, w_router):
        n_micro, tok, width = tokens.shape
        top_k = expert_ids.shape[2]
        heads, hd = w_query.shape[1:]
        kv_heads = w_key.shape[1]
        experts = w_router.shape[1]
        own = experts // groups
        cap = 2 * tok * top_k // experts
        share = groups // kv_heads
        seq = groups * tok
        columns = [[r + share * y for y in range(kv_heads)] for r in range(share)]
        rows = [[r + share * y for r in range(share)] for y in range(kv_heads)]
        per_q = min(4, groups)
        n_blk = groups // per_q

        def swap(a, **kw):
            return lax.all_to_all(a, 'sp', 0, 0, tiled=True, **kw)

        def queries(m, x):
            return jnp.einsum('td,dhk->hkt', x, w_query, preferred_element_type=F32).astype(BF16)

        w_kv = jnp.concatenate([w_key, w_value], axis=2)
        kv = jnp.einsum('mtd,dhk->hmkt', tokens, w_kv, preferred_element_type=F32).astype(BF16)
        ranks = slot_ranks(expert_ids, experts, cap).reshape(n_micro, groups, own, tok).transpose(1, 0, 2, 3)
        mine = swap(kv, axis_index_groups=columns)
        q = queries(0, tokens[0])
        mine, q, ranks = lax.optimization_barrier((mine, q, ranks))
        ranks = swap(ranks)
        kv_held, q_held = [], []
        for m in range(n_micro):
            if m > 0:
                x, _ = lax.optimization_barrier((tokens[m], q))
                q = queries(m, x)
                q, _ = lax.optimization_barrier((q, q_held[-1]))
            gathered = lax.all_gather(mine[:, m], 'sp', axis=0, axis_index_groups=rows)
            kv_held.append(gathered.reshape(share, kv_heads, 2 * hd, tok))
            q_held.append(swap(q))

        hidden, buffers, gathered = [], None, []
        attn = attention(q_held[0], kv_held[0], 0, n_blk, per_q)
        for m in range(n_micro):
            o = swap(attn.reshape(groups, tok, hd))
            part = None
            last = m + 1 == n_micro
            if not last:
                cut = (5 * n_blk) // 8
                part = attention(q_held[m + 1], kv_held[m + 1], 0, cut, per_q)
            parts = 2 if last else 1
            *pieces, h, gate = project(o, w_out, tokens[m], expert_ids[m], w_router, parts, after=() if last else (part,))
            hidden.append(h)
            pieces = [lax.all_gather(piece, 'sp', axis=0, tiled=True) for piece in pieces]
            gates = swap(gate.reshape(groups, own, tok))
            gathered.append((pieces, gates))
            if not last:
                attn = attention(q_held[m + 1], kv_held[m + 1], cut, n_blk, per_q, into=part, after=(h,))
        for m in range(n_micro):
            pieces, gates = gathered[m]
            for c, piece in enumerate(pieces):
                buffers = expert_rows(piece, ranks, gates, m, cap, width, c, into=buffers, after=(attn,) if m == 0 else ())
        return jnp.stack(hidden), buffers

    return jax.shard_map(
        local_step,
        mesh=mesh,
        in_specs=(P('dp', 'sp', None), P('dp', 'sp', None), P(), P(), P(), P(), P()),
        out_specs=(P('dp', 'sp', None), P('dp', 'sp', None, None)),
        check_vma=False,
    )
```

time: 564 us -> 525 us (0.931)
  blocking collectives: 52.8 us -> 0 us
  Pallas kernels: 259 us -> 207 us
  waiting for transfers between devices: 147 us -> 184 us
  matrix products: 19.5 us -> 49.7 us
  local copies, waits for them, and re-layouts: 28.9 us -> 17.1 us
  starting transfers between devices: 37.6 us -> 46.5 us
    all_to_all x2 -> x0, blocking collectives: 52.8 us -> none  [swap(): return lax.all_to_all(a, 'sp', 0, 0, tiled=True, **kw)]
    pallas_call x7 -> x8, Pallas kernels: 259 us -> 207 us  [the longest x3 130 us: attention(): pl.pallas_call(functools.partial(attention_kernel, lo), grid=(hi - lo,),...]
    all_gather x4 -> x5, waiting for transfers between devices: 63 us -> 97 us  [the longest x3 97 us: local_step(): lax.all_gather(piece, 'sp', axis=0, tiled=True)]
    dot_general x2 -> x3, matrix products: 19.3 us -> 49.5 us  [the longest x2 43.3 us: queries(): jnp.einsum('td,dhk->hkt', x, w_query, preferred_element_type=F32)]
    all_to_all x4 -> x0, local copies, waits for them, and re-layouts: 8.99 us -> none  [swap(): return lax.all_to_all(a, 'sp', 0, 0, tiled=True, **kw)]
    all_to_all x7 -> x8, starting transfers between devices: 37.1 us -> 45.5 us  [swap(): return lax.all_to_all(a, 'sp', 0, 0, tiled=True, **kw)]
    all_to_all x7 -> x8, waiting for transfers between devices: 83.8 us -> 85.9 us  [swap(): return lax.all_to_all(a, 'sp', 0, 0, tiled=True, **kw)]
  transfers between devices with their start and end apart: 11 -> 13, of which waited for: 5 -> 6; matrix products, arithmetic and copies ran while one was open for 6% -> 10% of each run, Pallas kernels for 39% -> 34%
where the time goes in v2:
time: 525 us; the launch traced here: 521 us
  Pallas kernels  207 us (39%)
  waiting for transfers between devices  184 us (35%)
  matrix products  49.7 us (9%)
  starting transfers between devices  46.5 us (9%)
  local copies, waits for them, and re-layouts  17.1 us (3%)
  between operations  14.5 us (3%)
    pallas_call x3, Pallas kernels, attention(): pl.pallas_call(functools.partial(attention_kernel, lo), grid=(hi - lo,),...  130 us
    all_gather x3, waiting for transfers between devices, local_step(): lax.all_gather(piece, 'sp', axis=0, tiled=True)  97 us
    all_to_all x8, waiting for transfers between devices, swap(): return lax.all_to_all(a, 'sp', 0, 0, tiled=True, **kw)  85.9 us
    pallas_call x3, Pallas kernels, expert_rows(): pl.pallas_call(rows_kernel, grid=(sources // some,), in_specs=[pl.BlockSp...  50.8 us
    all_to_all x8, starting transfers between devices, swap(): return lax.all_to_all(a, 'sp', 0, 0, tiled=True, **kw)  45.5 us
    dot_general x2, matrix products, queries(): jnp.einsum('td,dhk->hkt', x, w_query, preferred_element_type=F32)  43.3 us
    pallas_call x2, Pallas kernels, project(): pl.pallas_call(functools.partial(project_kernel, heads_blk, parts), grid=...  26 us
    unnamed x32, local copies, waits for them, and re-layouts  12.5 us
  transfers between devices with their start and end apart: 13, of which 6 were waited for; matrix products, arithmetic and copies ran while one was open for 10% of the time, Pallas kernels for 34%

profile of v2, /device:TPU:97, one launch (start us, length us, event | category | flops | bytes accessed | tf_op | source)
XLA Modules:
  0.0 521.4 jit_solution(16857039796755006916)
XLA Ops:
  7.2 4.4 copy.40
  11.6 2.6 copy.41
  14.1 6.2 %fusion.17 = bf16[4,2,256,256]{3,2,1,0:T(8,128)(2,1)} fusion(bf16[2,256,2048]{2,1,0:T(8,128)(2,1)} %param.7, bf16[2048,4,128]{0,2,1:T(8,128)(2,1)} %copy.41, bf16[2048,4,128]{0,2,1:T(8,128)(2,1)} %copy.40), kind=kOutput, calls=%fused_computation.15 | convolution fusion | flops 2156396544 | bytes 7340032 | tf_op jit(solution)/shard_map/mtd,dhk->hmkt/dot_general | solution.py:229
  20.4 6.6 %all-to-all-start = ((bf16[4,2,256,256]{3,2,1,0:T(8,128)(2,1)}), bf16[4,2,256,256]{3,2,1,0:T(8,128)(2,1)S(1)}, u32[]{:S(2)}, u32[]{:S(2)}) async-start(bf16[4,2,256,256]{3,2,1,0:T(8,128)(2,1)} %fusion.17), calls=%async_computation | async-start | bytes 2097152 | tf_op jit(solution)/shard_map/all_to_all | solution.py:223
  27.0 0.5 all-gather.14.cloned.1.call-start
  27.5 0.8 fusion.8
  28.4 0.2 and_select_fusion
  28.6 0.2 copy.43
  28.8 0.8 copy.62
  29.6 25.1 %fusion.11 = bf16[32,128,256]{2,1,0:T(8,128)(2,1)} fusion(bf16[2048,32,128]{2,1,0:T(8,128)(2,1)} %param.9, bf16[2,256,2048]{2,1,0:T(8,128)(2,1)S(1)} %copy-done.5), kind=kOutput, calls=%fused_computation.13 | convolution fusion | flops 4296015872 | bytes 19922944 | tf_op jit(solution)/shard_map/td,dhk->hkt/dot_general | solution.py:226
  54.7 1.1 fusion.29
  55.8 0.1 all-gather.16.cloned.1.call-start
  55.9 0.7 all-gather.16.cloned.1.call-update
  56.6 8.2 %all-to-all-start.1 = ((bf16[32,128,256]{2,1,0:T(8,128)(2,1)}), bf16[32,128,256]{2,1,0:T(8,128)(2,1)}, u32[]{:S(2)}, u32[]{:S(2)}) async-start(bf16[32,128,256]{2,1,0:T(8,128)(2,1)} %fusion.11), calls=%async_computation.1 | async-start | bytes 4194304 | tf_op jit(solution)/shard_map/all_to_all | solution.py:223
  64.8 1.2 slice_bitcast_fusion.1
  66.0 18.2 %convert_bitcast_fusion = bf16[32,128,256]{2,1,0:T(8,128)(2,1)} fusion(bf16[2048,32,128]{2,1,0:T(8,128)(2,1)} %param.9, bf16[256,2048]{1,0:T(8,128)(2,1)S(1)} %get-tuple-element.16.x_ref), kind=kOutput, calls=%fused_computation.10 | convolution fusion | flops 4296015872 | bytes 19922944 | tf_op jit(solution)/shard_map/td,dhk->hkt/dot_general | solution.py:226
  84.1 23.8 %all-to-all-done.1.q_ref = bf16[32,128,256]{2,1,0:T(8,128)(2,1)} async-done(((bf16[32,128,256]{2,1,0:T(8,128)(2,1)}), bf16[32,128,256]{2,1,0:T(8,128)(2,1)}, u32[]{:S(2)}, u32[]{:S(2)}) %all-to-all-start.1) | async-done | bytes 2097184 | tf_op jit(solution)/shard_map/all_to_all | solution.py:223
  107.9 4.8 all-to-all-start.3
  112.7 63.5 %attend.3 = bf16[8192,128]{1,0:T(8,128)(2,1)} custom-call(bf16[32,128,256]{2,1,0:T(8,128)(2,1)} %all-to-all-done.1.q_ref, bf16[8,4,256,256]{3,2,1,0:T(8,128)(2,1)} %bitcast.57), custom_call_target="tpu_custom_call" | custom-call | flops 34359738368 | bytes 8388608 | tf_op jit(solution)/shard_map/attend/pallas_call | solution.py:73
  176.3 1.3 copy-done.6
  177.6 6.6 %all-to-all-start.2 = ((bf16[32,256,128]{2,1,0:T(8,128)(2,1)}), bf16[32,256,128]{2,1,0:T(8,128)(2,1)S(1)}, u32[]{:S(2)}, u32[]{:S(2)}) async-start(bf16[32,256,128]{2,1,0:T(8,128)(2,1)} %bitcast.49), calls=%async_computation.2 | async-start | bytes 4194304 | tf_op jit(solution)/shard_map/all_to_all | solution.py:223
  184.2 0.1 all-gather.12.cloned.1.call-start
  184.3 0.8 copy.51
  185.1 28.1 %attend.4.rest_0_.rest_1_ = bf16[8192,128]{1,0:T(8,128)(2,1)} custom-call(bf16[32,128,256]{2,1,0:T(8,128)(2,1)} %copy-done.6, bf16[8,4,256,256]{3,2,1,0:T(8,128)(2,1)} %bitcast.55), custom_call_target="tpu_custom_call" | custom-call | flops 13421772800 | bytes 8388608 | tf_op jit(solution)/shard_map/attend/pallas_call | solution.py:73
  213.2 1.3 copy-done.1
  214.5 13.0 %project.2 = (bf16[256,2048]{1,0:T(8,128)(2,1)}, bf16[256,2048]{1,0:T(8,128)(2,1)}, f32[128,256]{1,0:T(8,128)}) custom-call(bf16[32,256,128]{2,1,0:T(8,128)(2,1)} %copy-done.1, bf16[32,128,2048]{2,1,0:T(8,128)(2,1)} %w_ref.3, bf16[256,2048]{1,0:T(8,128)(2,1)} %get-tuple-element.26.x_ref, s32[256,8]{1,0:T(8,128)} %bitcast.53, bf16[2048,128]{1,0:T(8,128)(2,1)} %wr_ref.3, ...), custom_call_target="tpu_custom_call" | custom-call | flops 4294967296 | bytes 16777216 | tf_op jit(solution)/shard_map/project/pallas_call | solution.py:130
  227.6 38.4 %attend.5.rest_0_ = bf16[8192,128]{1,0:T(8,128)(2,1)} custom-call(bf16[32,128,256]{2,1,0:T(8,128)(2,1)} %copy-done.6, bf16[8,4,256,256]{3,2,1,0:T(8,128)(2,1)} %bitcast.56, bf16[256,2048]{1,0:T(8,128)(2,1)} %get-tuple-element.18.rest_0_, bf16[8192,128]{1,0:T(8,128)(2,1)} %attend.4.rest_0_.rest_1_), custom_call_target="tpu_custom_call", output_to_operand_aliasing={{}: (3, {})} | custom-call | flops 20937965568 | bytes 8388608 | tf_op jit(solution)/shard_map/attend/pallas_call | solution.py:73
  266.0 6.3 %all-to-all-start.4 = ((bf16[32,256,128]{2,1,0:T(8,128)(2,1)}), bf16[32,256,128]{2,1,0:T(8,128)(2,1)S(1)}, u32[]{:S(2)}, u32[]{:S(2)}) async-start(bf16[32,256,128]{2,1,0:T(8,128)(2,1)} %bitcast.48), calls=%async_computation.4 | async-start | bytes 4194304 | tf_op jit(solution)/shard_map/all_to_all | solution.py:223
  272.3 0.4 all-gather.10.cloned.1.call-start
  272.7 0.8 copy.52
  273.5 45.9 %all-to-all-done.4.o_ref = bf16[32,256,128]{2,1,0:T(8,128)(2,1)S(1)} async-done(((bf16[32,256,128]{2,1,0:T(8,128)(2,1)}), bf16[32,256,128]{2,1,0:T(8,128)(2,1)S(1)}, u32[]{:S(2)}, u32[]{:S(2)}) %all-to-all-start.4) | async-done | bytes 2097184 | tf_op jit(solution)/shard_map/all_to_all | solution.py:223
  319.4 1.3 copy-done
  320.7 13.0 %project.3 = (bf16[256,1024]{1,0:T(8,128)(2,1)}, bf16[256,1024]{1,0:T(8,128)(2,1)}, bf16[256,2048]{1,0:T(8,128)(2,1)}, f32[128,256]{1,0:T(8,128)}) custom-call(bf16[32,256,128]{2,1,0:T(8,128)(2,1)} %copy-done, bf16[32,128,2048]{2,1,0:T(8,128)(2,1)} %w_ref.3, bf16[256,2048]{1,0:T(8,128)(2,1)} %copy-done.3, s32[256,8]{1,0:T(8,128)} %bitcast.54, ...), custom_call_target="tpu_custom_call" | custom-call | flops 4294967296 | bytes 16777216 | tf_op jit(solution)/shard_map/project/pallas_call | solution.py:130
  333.8 0.1 all-gather.8.cloned.1.call-start
  333.8 0.6 all-gather.8.cloned.1.call-update
  334.4 6.8 %all-to-all-start.5 = ((f32[32,2,4,256]{3,2,1,0:T(4,128)}), f32[32,2,4,256]{3,2,1,0:T(4,128)S(1)}, u32[]{:S(2)}, u32[]{:S(2)}) async-start(f32[32,2,4,256]{3,2,1,0:T(4,128)} %bitcast.47), calls=%async_computation.5 | async-start | bytes 524288 | tf_op jit(solution)/shard_map/all_to_all | solution.py:223
  341.2 0.7 reshape.24
  341.9 10.8 %all-to-all-done.5.rank_ref = f32[32,2,4,256]{3,2,1,0:T(4,128)S(1)} async-done(((f32[32,2,4,256]{3,2,1,0:T(4,128)}), f32[32,2,4,256]{3,2,1,0:T(4,128)S(1)}, u32[]{:S(2)}, u32[]{:S(2)}) %all-to-all-start.5) | async-done | bytes 262176 | tf_op jit(solution)/shard_map/all_to_all | solution.py:223
  352.7 3.4 all-to-all-start.7
  356.0 1.5 pad_maximum_fusion
  357.6 0.7 reshape.23
  358.2 5.4 %all-to-all-done.7.gate_ref = f32[32,4,256]{2,1,0:T(4,128)S(1)} async-done(((f32[32,4,256]{2,1,0:T(4,128)}), f32[32,4,256]{2,1,0:T(4,128)S(1)}, u32[]{:S(2)}, u32[]{:S(2)}) %all-to-all-start.7) | async-done | bytes 131104 | tf_op jit(solution)/shard_map/all_to_all | solution.py:223
  363.6 2.9 all-to-all-start.6
  366.6 21.8 %expert_rows.3.rest_0_ = bf16[2,4,1024,2048]{3,2,1,0:T(8,128)(2,1)} custom-call(bf16[8192,2048]{1,0:T(8,128)(2,1)} %all-gather.12.cloned.1.call-done.h_ref, f32[32,2,4,256]{3,2,1,0:T(4,128)} %copy-done.2, f32[32,4,256]{2,1,0:T(4,128)} %copy-done.10, bf16[8192,128]{1,0:T(8,128)(2,1)} %attend.5.rest_0_), custom_call_target="tpu_custom_call" | custom-call | flops 4294967296 | bytes 50331648 | tf_op jit(solution)/shard_map/expert_rows/pallas_call | solution.py:180
  388.3 42.8 %all-gather.10.cloned.1.call-done.h_ref = bf16[8192,1024]{1,0:T(8,128)(2,1)} async-done(((bf16[256,1024]{1,0:T(8,128)(2,1)}), bf16[8192,1024]{1,0:T(8,128)(2,1)}) %all-gather.10.cloned.1.call-update) | async-done | bytes 16777232 | tf_op jit(solution)/shard_map/all_gather | solution.py:257
  431.2 14.5 %expert_rows.4.rest_0_ = bf16[2,4,1024,2048]{3,2,1,0:T(8,128)(2,1)} custom-call(bf16[8192,1024]{1,0:T(8,128)(2,1)} %all-gather.10.cloned.1.call-done.h_ref, f32[32,2,4,256]{3,2,1,0:T(4,128)} %copy-done.2, f32[32,4,256]{2,1,0:T(4,128)} %copy-done.7, bf16[2,4,1024,2048]{3,2,1,0:T(8,128)(2,1)} %expert_rows.3.rest_0_), custom_call_target="tpu_custom_call", output_to_operand_aliasing={{}: (3, {})} | custom-call | flops 2147483648 | bytes 25165824 | tf_op jit(solution)/shard_map/expert_rows/pallas_call | solution.py:180
  445.7 54.1 %all-gather.8.cloned.1.call-done.h_ref = bf16[8192,1024]{1,0:T(8,128)(2,1)} async-done(((bf16[256,1024]{1,0:T(8,128)(2,1)}), bf16[8192,1024]{1,0:T(8,128)(2,1)}) %all-gather.8.cloned.1.call-update) | async-done | bytes 16777232 | tf_op jit(solution)/shard_map/all_gather | solution.py:257
  499.8 14.5 %expert_rows.5 = bf16[2,4,1024,2048]{3,2,1,0:T(8,128)(2,1)} custom-call(bf16[8192,1024]{1,0:T(8,128)(2,1)} %all-gather.8.cloned.1.call-done.h_ref, f32[32,2,4,256]{3,2,1,0:T(4,128)} %copy-done.2, f32[32,4,256]{2,1,0:T(4,128)} %copy-done.7, bf16[2,4,1024,2048]{3,2,1,0:T(8,128)(2,1)} %expert_rows.4.rest_0_), custom_call_target="tpu_custom_call", output_to_operand_aliasing={{}: (3, {})} | custom-call | flops 2147483648 | bytes 25165824 | tf_op jit(solution)/shard_map/expert_rows/pallas_call | solution.py:180
  (36 shorter events, 0.3 us)
Async XLA Ops:
  7.2 4.4 copy-start.4
  14.1 13.4 %copy-start.13 = (s32[2,256,8]{1,2,0:T(8,128)S(1)}, s32[2,256,8]{1,2,0:T(8,128)}, u32[]{:S(2)}) copy-start(s32[2,256,8]{1,2,0:T(8,128)} %param.8) | copy-start | bytes 49156
  20.4 9.2 %copy-start.5 = (bf16[2,256,2048]{2,1,0:T(8,128)(2,1)S(1)}, bf16[2,256,2048]{2,1,0:T(8,128)(2,1)}, u32[]{:S(2)}) copy-start(bf16[2,256,2048]{2,1,0:T(8,128)(2,1)} %param.7) | copy-start | bytes 6291460
  20.4 34.3 %all-to-all-start = ((bf16[4,2,256,256]{3,2,1,0:T(8,128)(2,1)}), bf16[4,2,256,256]{3,2,1,0:T(8,128)(2,1)S(1)}, u32[]{:S(2)}, u32[]{:S(2)}) async-start(bf16[4,2,256,256]{3,2,1,0:T(8,128)(2,1)} %fusion.17), calls=%async_computation | async-start | bytes 2097152 | tf_op jit(solution)/shard_map/all_to_all | solution.py:223
  27.0 85.7 %all-gather.14.cloned.1.call-start = ((), (), s32[]{:S(2)}) async-start(), calls=%async_computation.11 | async-start | bytes 4718592 | tf_op jit(solution)/shard_map/all_gather | solution.py:241
  55.8 129.2 %all-gather.16.cloned.1.call-start = ((), (), s32[]{:S(2)}) async-start(), calls=%async_computation.12 | async-start | bytes 4718592 | tf_op jit(solution)/shard_map/all_gather | solution.py:241
  56.6 51.3 %all-to-all-start.1 = ((bf16[32,128,256]{2,1,0:T(8,128)(2,1)}), bf16[32,128,256]{2,1,0:T(8,128)(2,1)}, u32[]{:S(2)}, u32[]{:S(2)}) async-start(bf16[32,128,256]{2,1,0:T(8,128)(2,1)} %fusion.11), calls=%async_computation.1 | async-start | bytes 4194304 | tf_op jit(solution)/shard_map/all_to_all | solution.py:223
  66.0 18.2 %copy-start.3 = (bf16[256,2048]{1,0:T(8,128)(2,1)}, bf16[256,2048]{1,0:T(8,128)(2,1)S(1)}, u32[]{:S(2)}) copy-start(bf16[256,2048]{1,0:T(8,128)(2,1)S(1)} %get-tuple-element.16.x_ref) | copy-start | bytes 3145732
  107.9 68.3 %all-to-all-start.3 = ((bf16[32,128,256]{2,1,0:T(8,128)(2,1)}), bf16[32,128,256]{2,1,0:T(8,128)(2,1)S(1)}, u32[]{:S(2)}, u32[]{:S(2)}) async-start(bf16[32,128,256]{2,1,0:T(8,128)(2,1)} %convert_bitcast_fusion), calls=%async_computation.3 | async-start | bytes 4194304 | tf_op jit(solution)/shard_map/all_to_all | solution.py:223
  176.3 1.3 copy-start.6
  177.6 35.6 %all-to-all-start.2 = ((bf16[32,256,128]{2,1,0:T(8,128)(2,1)}), bf16[32,256,128]{2,1,0:T(8,128)(2,1)S(1)}, u32[]{:S(2)}, u32[]{:S(2)}) async-start(bf16[32,256,128]{2,1,0:T(8,128)(2,1)} %bitcast.49), calls=%async_computation.2 | async-start | bytes 4194304 | tf_op jit(solution)/shard_map/all_to_all | solution.py:223
  184.2 182.3 %all-gather.12.cloned.1.call-start = ((), (), s32[]{:S(2)}) async-start(), calls=%async_computation.10 | async-start | bytes 34603008 | tf_op jit(solution)/shard_map/all_gather | solution.py:257
  213.2 1.3 copy-start.1
  266.0 53.4 %all-to-all-start.4 = ((bf16[32,256,128]{2,1,0:T(8,128)(2,1)}), bf16[32,256,128]{2,1,0:T(8,128)(2,1)S(1)}, u32[]{:S(2)}, u32[]{:S(2)}) async-start(bf16[32,256,128]{2,1,0:T(8,128)(2,1)} %bitcast.48), calls=%async_computation.4 | async-start | bytes 4194304 | tf_op jit(solution)/shard_map/all_to_all | solution.py:223
  272.3 158.9 %all-gather.10.cloned.1.call-start = ((), (), s32[]{:S(2)}) async-start(), calls=%async_computation.9 | async-start | bytes 17301504 | tf_op jit(solution)/shard_map/all_gather | solution.py:257
  319.4 1.3 copy-start
  320.7 20.5 %copy-start.11 = (f32[128,256]{1,0:T(8,128)S(1)}, f32[128,256]{1,0:T(8,128)}, u32[]{:S(2)}) copy-start(f32[128,256]{1,0:T(8,128)} %get-tuple-element.25) | copy-start | bytes 393220
  333.7 22.3 %copy-start.8 = (bf16[256,2048]{1,0:T(8,128)(2,1)S(1)}, bf16[256,2048]{1,0:T(8,128)(2,1)}, u32[]{:S(2)}) copy-start(bf16[256,2048]{1,0:T(8,128)(2,1)} %get-tuple-element.18.rest_0_) | copy-start | bytes 3145732
  333.7 22.3 %copy-start.9 = (bf16[256,2048]{1,0:T(8,128)(2,1)S(1)}, bf16[256,2048]{1,0:T(8,128)(2,1)}, u32[]{:S(2)}) copy-start(bf16[256,2048]{1,0:T(8,128)(2,1)} %get-tuple-element.19) | copy-start | bytes 3145732
  333.8 166.0 %all-gather.8.cloned.1.call-start = ((), (), s32[]{:S(2)}) async-start(), calls=%async_computation.8 | async-start | bytes 17301504 | tf_op jit(solution)/shard_map/all_gather | solution.py:257
  334.4 18.2 %all-to-all-start.5 = ((f32[32,2,4,256]{3,2,1,0:T(4,128)}), f32[32,2,4,256]{3,2,1,0:T(4,128)S(1)}, u32[]{:S(2)}, u32[]{:S(2)}) async-start(f32[32,2,4,256]{3,2,1,0:T(4,128)} %bitcast.47), calls=%async_computation.5 | async-start | bytes 524288 | tf_op jit(solution)/shard_map/all_to_all | solution.py:223
  352.7 4.9 copy-start.2
  352.7 11.0 %all-to-all-start.7 = ((f32[32,4,256]{2,1,0:T(4,128)}), f32[32,4,256]{2,1,0:T(4,128)S(1)}, u32[]{:S(2)}, u32[]{:S(2)}) async-start(f32[32,4,256]{2,1,0:T(4,128)} %reshape.24), calls=%async_computation.7 | async-start | bytes 262144 | tf_op jit(solution)/shard_map/all_to_all | solution.py:223
  356.0 1.5 copy-start.12
  363.6 2.9 copy-start.10
  363.6 24.7 %all-to-all-start.6 = ((f32[32,4,256]{2,1,0:T(4,128)}), f32[32,4,256]{2,1,0:T(4,128)S(1)}, u32[]{:S(2)}, u32[]{:S(2)}) async-start(f32[32,4,256]{2,1,0:T(4,128)} %reshape.23), calls=%async_computation.6 | async-start | bytes 262144 | tf_op jit(solution)/shard_map/all_to_all | solution.py:223
  388.3 42.8 %copy-start.7 = (f32[32,4,256]{2,1,0:T(4,128)}, f32[32,4,256]{2,1,0:T(4,128)S(1)}, u32[]{:S(2)}) copy-start(f32[32,4,256]{2,1,0:T(4,128)S(1)} %all-to-all-done.6.gate_ref) | copy-start | bytes 393220
Sparse Core Ops, SparseCore 0:
  56.0 52.5 all-gather.13
  110.2 47.0 all-gather.15
  227.7 134.9 all-gather.11
  364.6 66.4 all-gather.9
  433.1 66.6 all-gather.7

commit v3 on v2

--- a/solution.py
+++ b/solution.py
@@ -222,21 +222,17 @@
         def swap(a, **kw):
             return lax.all_to_all(a, 'sp', 0, 0, tiled=True, **kw)
 
-        def queries(m, x):
-            return jnp.einsum('td,dhk->hkt', x, w_query, preferred_element_type=F32).astype(BF16)
-
         w_kv = jnp.concatenate([w_key, w_value], axis=2)
         kv = jnp.einsum('mtd,dhk->hmkt', tokens, w_kv, preferred_element_type=F32).astype(BF16)
         ranks = slot_ranks(expert_ids, experts, cap).reshape(n_micro, groups, own, tok).transpose(1, 0, 2, 3)
         mine = swap(kv, axis_index_groups=columns)
-        q = queries(0, tokens[0])
-        mine, q, ranks = lax.optimization_barrier((mine, q, ranks))
+        queries = jnp.einsum('mtd,dhk->hmkt', tokens, w_query, preferred_element_type=F32).astype(BF16)
+        mine, queries, ranks = lax.optimization_barrier((mine, queries, ranks))
         ranks = swap(ranks)
         kv_held, q_held = [], []
         for m in range(n_micro):
+            q = queries[:, m]
             if m > 0:
-                x, _ = lax.optimization_barrier((tokens[m], q))
-                q = queries(m, x)
                 q, _ = lax.optimization_barrier((q, q_held[-1]))
             gathered = lax.all_gather(mine[:, m], 'sp', axis=0, axis_index_groups=rows)
             kv_held.append(gathered.reshape(share, kv_heads, 2 * hd, tok))
@@ -251,7 +247,7 @@
             if not last:
                 cut = (5 * n_blk) // 8
                 part = attention(q_held[m + 1], kv_held[m + 1], 0, cut, per_q)
-            parts = 2 if last else 1
+            parts = 1
             *pieces, h, gate = project(o, w_out, tokens[m], expert_ids[m], w_router, parts, after=() if last else (part,))
             hidden.append(h)
             pieces = [lax.all_gather(piece, 'sp', axis=0, tiled=True) for piece in pieces]

time: 525 us -> 519 us (0.989)
  blocking collectives: 0 us -> 49.3 us
  waiting for transfers between devices: 184 us -> 148 us
  local copies, waits for them, and re-layouts: 17.1 us -> 47.1 us
  matrix products: 49.7 us -> 20.4 us
  starting transfers between devices: 46.5 us -> 37.1 us
  Pallas kernels: 207 us -> 200 us
    all_to_all x0 -> x1, blocking collectives: none -> 49.3 us  [swap(): return lax.all_to_all(a, 'sp', 0, 0, tiled=True, **kw)]
    dot_general x2 -> x1, matrix products: 43.3 us -> 14 us  [local_step(): jnp.einsum('mtd,dhk->hmkt', tokens, w_query, preferred_element_type=F32)]
    unnamed x32 -> x31, local copies, waits for them, and re-layouts: 12.5 us -> 36.5 us
    all_to_all x8 -> x7, waiting for transfers between devices: 85.9 us -> 62.4 us  [swap(): return lax.all_to_all(a, 'sp', 0, 0, tiled=True, **kw)]
    all_gather x3 -> x2, waiting for transfers between devices: 97 us -> 84.8 us  [local_step(): lax.all_gather(piece, 'sp', axis=0, tiled=True)]
    all_to_all x8 -> x7, starting transfers between devices: 45.5 us -> 36.6 us  [swap(): return lax.all_to_all(a, 'sp', 0, 0, tiled=True, **kw)]
    pallas_call x3 -> x2, Pallas kernels: 50.8 us -> 43.5 us  [expert_rows(): pl.pallas_call(rows_kernel, grid=(sources // some,), in_specs=[pl.BlockSp...]
    squeeze x1 -> x2, local copies, waits for them, and re-layouts: 1.16 us -> 7.15 us  [the longest x1 4.04 us: local_step(): q = queries[:, m]]
  transfers between devices with their start and end apart: 13 -> 11, of which waited for: 6 -> 4; matrix products, arithmetic and copies ran while one was open for 10% -> 10% of each run, Pallas kernels for 34% -> 32%
where the time goes in v3:
time: 519 us; the launch traced here: 518 us
  Pallas kernels  200 us (39%)
  waiting for transfers between devices  148 us (29%)
  blocking collectives  49.3 us (9%)
  local copies, waits for them, and re-layouts  47.1 us (9%)
  starting transfers between devices  37.1 us (7%)
  matrix products  20.4 us (4%)
  between operations  13.9 us (3%)
    pallas_call x3, Pallas kernels, attention(): pl.pallas_call(functools.partial(attention_kernel, lo), grid=(hi - lo,),...  130 us
    all_gather x2, waiting for transfers between devices, local_step(): lax.all_gather(piece, 'sp', axis=0, tiled=True)  84.8 us
    all_to_all x7, waiting for transfers between devices, swap(): return lax.all_to_all(a, 'sp', 0, 0, tiled=True, **kw)  62.4 us
    all_to_all x1, blocking collectives, swap(): return lax.all_to_all(a, 'sp', 0, 0, tiled=True, **kw)  49.3 us
    pallas_call x2, Pallas kernels, expert_rows(): pl.pallas_call(rows_kernel, grid=(sources // some,), in_specs=[pl.BlockSp...  43.5 us
    all_to_all x7, starting transfers between devices, swap(): return lax.all_to_all(a, 'sp', 0, 0, tiled=True, **kw)  36.6 us
    unnamed x31, local copies, waits for them, and re-layouts  36.5 us
    pallas_call x2, Pallas kernels, project(): pl.pallas_call(functools.partial(project_kernel, heads_blk, parts), grid=...  26.1 us
  transfers between devices with their start and end apart: 11, of which 4 were waited for; matrix products, arithmetic and copies ran while one was open for 10% of the time, Pallas kernels for 32%

profile of v3, /device:TPU:97, one launch (start us, length us, event | category | flops | bytes accessed | tf_op | source)
XLA Modules:
  0.0 517.9 jit_solution(11733798987122451820)
XLA Ops:
  7.2 4.4 copy.36
  11.6 2.6 copy.37
  14.1 6.2 %fusion.13 = bf16[4,2,256,256]{3,2,1,0:T(8,128)(2,1)} fusion(bf16[2,256,2048]{2,1,0:T(8,128)(2,1)} %param.7, bf16[2048,4,128]{0,2,1:T(8,128)(2,1)} %copy.37, bf16[2048,4,128]{0,2,1:T(8,128)(2,1)} %copy.36), kind=kOutput, calls=%fused_computation.15 | convolution fusion | flops 2156396544 | bytes 7340032 | tf_op jit(solution)/shard_map/mtd,dhk->hmkt/dot_general | solution.py:226
  20.4 6.5 %all-to-all-start = ((bf16[4,2,256,256]{3,2,1,0:T(8,128)(2,1)}), bf16[4,2,256,256]{3,2,1,0:T(8,128)(2,1)S(1)}, u32[]{:S(2)}, u32[]{:S(2)}) async-start(bf16[4,2,256,256]{3,2,1,0:T(8,128)(2,1)} %fusion.13), calls=%async_computation | async-start | bytes 2097152 | tf_op jit(solution)/shard_map/all_to_all | solution.py:223
  26.9 24.0 %copy.38 = bf16[2048,32,128]{0,2,1:T(8,128)(2,1)} copy(bf16[2048,32,128]{2,1,0:T(8,128)(2,1)} %param.9) | data formatting | bytes 33554432 | tf_op args[2]
  50.9 14.0 %convert_bitcast_fusion = bf16[32,2,128,256]{3,2,0,1:T(8,128)(2,1)} fusion(bf16[2048,32,128]{0,2,1:T(8,128)(2,1)} %copy.38, bf16[2,256,2048]{2,1,0:T(8,128)(2,1)S(1)} %copy-done.4), kind=kOutput, calls=%fused_computation.6 | convolution fusion | flops 8592031744 | bytes 23068672 | tf_op jit(solution)/shard_map/mtd,dhk->hmkt/dot_general | solution.py:229
  64.8 0.8 fusion.9
  65.7 0.2 and_select_fusion
  65.9 0.2 copy.40
  66.1 0.8 copy.50
  66.9 1.1 fusion.22
  68.0 0.1 all-gather.11.cloned.1.call-update
  68.0 0.1 all-gather.13.cloned.1.call-start
  68.1 0.7 all-gather.13.cloned.1.call-update
  68.8 4.0 slice_bitcast_fusion.1
  72.9 49.3 %all_to_all.40.q_ref = bf16[32,128,256]{2,1,0:T(8,128)(2,1)} all-to-all(bf16[32,128,256]{2,1,0:T(8,128)(2,1)S(1)} %get-tuple-element.22), channel_id=1, replica_groups=mesh['dp'=1,'sp'=32] {'sp'}, dimensions={0} | all-to-all | bytes 4194304 | tf_op jit(solution)/shard_map/all_to_all | solution.py:223
  122.1 4.0 all-to-all-start.3
  126.2 0.0 all-gather.11.cloned.1.call-done
  126.2 63.5 %attend.3 = bf16[8192,128]{1,0:T(8,128)(2,1)} custom-call(bf16[32,128,256]{2,1,0:T(8,128)(2,1)} %all_to_all.40.q_ref, bf16[8,4,256,256]{3,2,1,0:T(8,128)(2,1)} %bitcast.64), custom_call_target="tpu_custom_call" | custom-call | flops 34359738368 | bytes 8388608 | tf_op jit(solution)/shard_map/attend/pallas_call | solution.py:73
  189.7 1.3 copy-done.5
  191.1 6.7 %all-to-all-start.2 = ((bf16[32,256,128]{2,1,0:T(8,128)(2,1)}), bf16[32,256,128]{2,1,0:T(8,128)(2,1)S(1)}, u32[]{:S(2)}, u32[]{:S(2)}) async-start(bf16[32,256,128]{2,1,0:T(8,128)(2,1)} %bitcast.56), calls=%async_computation.2 | async-start | bytes 4194304 | tf_op jit(solution)/shard_map/all_to_all | solution.py:223
  197.8 0.1 all-gather.9.cloned.1.call-start
  197.9 0.8 copy.47
  198.6 3.1 slice_bitcast_fusion.2
  201.8 28.1 %attend.4.rest_0_.rest_1_ = bf16[8192,128]{1,0:T(8,128)(2,1)} custom-call(bf16[32,128,256]{2,1,0:T(8,128)(2,1)} %copy-done.5, bf16[8,4,256,256]{3,2,1,0:T(8,128)(2,1)} %bitcast.62), custom_call_target="tpu_custom_call" | custom-call | flops 13421772800 | bytes 8388608 | tf_op jit(solution)/shard_map/attend/pallas_call | solution.py:73
  229.9 1.3 copy-done.1
  231.2 13.1 %project.2 = (bf16[256,2048]{1,0:T(8,128)(2,1)}, bf16[256,2048]{1,0:T(8,128)(2,1)}, f32[128,256]{1,0:T(8,128)}) custom-call(bf16[32,256,128]{2,1,0:T(8,128)(2,1)} %copy-done.1, bf16[32,128,2048]{2,1,0:T(8,128)(2,1)} %w_ref.3, bf16[256,2048]{1,0:T(8,128)(2,1)} %get-tuple-element.25.x_ref, s32[256,8]{1,0:T(8,128)} %bitcast.60, bf16[2048,128]{1,0:T(8,128)(2,1)} %wr_ref.3, ...), custom_call_target="tpu_custom_call" | custom-call | flops 4294967296 | bytes 16777216 | tf_op jit(solution)/shard_map/project/pallas_call | solution.py:130
  244.3 0.1 all-gather.9.cloned.1.call-update
  244.3 38.4 %attend.5.rest_0_ = bf16[8192,128]{1,0:T(8,128)(2,1)} custom-call(bf16[32,128,256]{2,1,0:T(8,128)(2,1)} %copy-done.5, bf16[8,4,256,256]{3,2,1,0:T(8,128)(2,1)} %bitcast.63, bf16[256,2048]{1,0:T(8,128)(2,1)} %get-tuple-element.15.rest_0_, bf16[8192,128]{1,0:T(8,128)(2,1)} %attend.4.rest_0_.rest_1_), custom_call_target="tpu_custom_call", output_to_operand_aliasing={{}: (3, {})} | custom-call | flops 20937965568 | bytes 8388608 | tf_op jit(solution)/shard_map/attend/pallas_call | solution.py:73
  282.7 6.3 %all-to-all-start.4 = ((bf16[32,256,128]{2,1,0:T(8,128)(2,1)}), bf16[32,256,128]{2,1,0:T(8,128)(2,1)S(1)}, u32[]{:S(2)}, u32[]{:S(2)}) async-start(bf16[32,256,128]{2,1,0:T(8,128)(2,1)} %bitcast.55), calls=%async_computation.4 | async-start | bytes 4194304 | tf_op jit(solution)/shard_map/all_to_all | solution.py:223
  289.0 0.3 all-gather.7.cloned.1.call-start
  289.3 0.8 copy.48
  290.1 46.0 %all-to-all-done.4.o_ref = bf16[32,256,128]{2,1,0:T(8,128)(2,1)S(1)} async-done(((bf16[32,256,128]{2,1,0:T(8,128)(2,1)}), bf16[32,256,128]{2,1,0:T(8,128)(2,1)S(1)}, u32[]{:S(2)}, u32[]{:S(2)}) %all-to-all-start.4) | async-done | bytes 2097184 | tf_op jit(solution)/shard_map/all_to_all | solution.py:223
  336.1 1.3 copy-done
  337.4 13.0 %project.3 = (bf16[256,2048]{1,0:T(8,128)(2,1)}, bf16[256,2048]{1,0:T(8,128)(2,1)}, f32[128,256]{1,0:T(8,128)}) custom-call(bf16[32,256,128]{2,1,0:T(8,128)(2,1)} %copy-done, bf16[32,128,2048]{2,1,0:T(8,128)(2,1)} %w_ref.3, bf16[256,2048]{1,0:T(8,128)(2,1)} %get-tuple-element.24.x_ref, s32[256,8]{1,0:T(8,128)} %bitcast.61, bf16[2048,128]{1,0:T(8,128)(2,1)} %wr_ref.3), custom_call_target="tpu_custom_call" | custom-call | flops 4294967296 | bytes 16777216 | tf_op jit(solution)/shard_map/project/pallas_call | solution.py:130
  350.4 0.1 all-gather.7.cloned.1.call-update
  350.5 6.9 %all-to-all-start.5 = ((f32[32,2,4,256]{3,2,1,0:T(4,128)}), f32[32,2,4,256]{3,2,1,0:T(4,128)S(1)}, u32[]{:S(2)}, u32[]{:S(2)}) async-start(f32[32,2,4,256]{3,2,1,0:T(4,128)} %bitcast.54), calls=%async_computation.5 | async-start | bytes 524288 | tf_op jit(solution)/shard_map/all_to_all | solution.py:223
  357.4 0.7 reshape.24
  358.1 10.8 %all-to-all-done.5.rank_ref = f32[32,2,4,256]{3,2,1,0:T(4,128)S(1)} async-done(((f32[32,2,4,256]{3,2,1,0:T(4,128)}), f32[32,2,4,256]{3,2,1,0:T(4,128)S(1)}, u32[]{:S(2)}, u32[]{:S(2)}) %all-to-all-start.5) | async-done | bytes 262176 | tf_op jit(solution)/shard_map/all_to_all | solution.py:223
  368.9 3.3 all-to-all-start.7
  372.2 1.5 pad_maximum_fusion
  373.8 0.7 reshape.23
  374.4 5.7 %all-to-all-done.7.gate_ref = f32[32,4,256]{2,1,0:T(4,128)S(1)} async-done(((f32[32,4,256]{2,1,0:T(4,128)}), f32[32,4,256]{2,1,0:T(4,128)S(1)}, u32[]{:S(2)}, u32[]{:S(2)}) %all-to-all-start.7) | async-done | bytes 131104 | tf_op jit(solution)/shard_map/all_to_all | solution.py:223
  380.1 2.9 all-to-all-start.6
  383.0 0.0 all-gather.9.cloned.1.call-done.h_ref
  383.0 21.8 %expert_rows.2.rest_0_ = bf16[2,4,1024,2048]{3,2,1,0:T(8,128)(2,1)} custom-call(bf16[8192,2048]{1,0:T(8,128)(2,1)} %all-gather.9.cloned.1.call-done.h_ref, f32[32,2,4,256]{3,2,1,0:T(4,128)} %copy-done.2, f32[32,4,256]{2,1,0:T(4,128)} %copy-done.8, bf16[8192,128]{1,0:T(8,128)(2,1)} %attend.5.rest_0_), custom_call_target="tpu_custom_call" | custom-call | flops 4294967296 | bytes 50331648 | tf_op jit(solution)/shard_map/expert_rows/pallas_call | solution.py:180
  404.8 84.8 %all-gather.7.cloned.1.call-done.h_ref = bf16[8192,2048]{1,0:T(8,128)(2,1)} async-done(((bf16[256,2048]{1,0:T(8,128)(2,1)}), bf16[8192,2048]{1,0:T(8,128)(2,1)}) %all-gather.7.cloned.1.call-update) | async-done | bytes 33554448 | tf_op jit(solution)/shard_map/all_gather | solution.py:253
  489.6 21.7 %expert_rows.3 = bf16[2,4,1024,2048]{3,2,1,0:T(8,128)(2,1)} custom-call(bf16[8192,2048]{1,0:T(8,128)(2,1)} %all-gather.7.cloned.1.call-done.h_ref, f32[32,2,4,256]{3,2,1,0:T(4,128)} %copy-done.2, f32[32,4,256]{2,1,0:T(4,128)} %copy-done.9, bf16[2,4,1024,2048]{3,2,1,0:T(8,128)(2,1)} %expert_rows.2.rest_0_), custom_call_target="tpu_custom_call", output_to_operand_aliasing={{}: (3, {})} | custom-call | flops 4294967296 | bytes 50331648 | tf_op jit(solution)/shard_map/expert_rows/pallas_call | solution.py:180
  (30 shorter events, 0.1 us)
Async XLA Ops:
  7.2 4.4 copy-start.3
  20.4 46.5 %all-to-all-start = ((bf16[4,2,256,256]{3,2,1,0:T(8,128)(2,1)}), bf16[4,2,256,256]{3,2,1,0:T(8,128)(2,1)S(1)}, u32[]{:S(2)}, u32[]{:S(2)}) async-start(bf16[4,2,256,256]{3,2,1,0:T(8,128)(2,1)} %fusion.13), calls=%async_computation | async-start | bytes 2097152 | tf_op jit(solution)/shard_map/all_to_all | solution.py:223
  26.9 24.0 %copy-start.4 = (bf16[2,256,2048]{2,1,0:T(8,128)(2,1)S(1)}, bf16[2,256,2048]{2,1,0:T(8,128)(2,1)}, u32[]{:S(2)}) copy-start(bf16[2,256,2048]{2,1,0:T(8,128)(2,1)} %param.7) | copy-start | bytes 6291460
  26.9 99.4 %all-gather.11.cloned.1.call-start = ((), (), s32[]{:S(2)}) async-start(), calls=%async_computation.10 | async-start | bytes 4718592 | tf_op jit(solution)/shard_map/all_gather | solution.py:237
  50.9 14.0 %copy-start.12 = (s32[2,256,8]{1,2,0:T(8,128)S(1)}, s32[2,256,8]{1,2,0:T(8,128)}, u32[]{:S(2)}) copy-start(s32[2,256,8]{1,2,0:T(8,128)} %param.8) | copy-start | bytes 49156
  68.0 133.7 %all-gather.13.cloned.1.call-start = ((), (), s32[]{:S(2)}) async-start(), calls=%async_computation.11 | async-start | bytes 4718592 | tf_op jit(solution)/shard_map/all_gather | solution.py:237
  122.1 67.6 %all-to-all-start.3 = ((bf16[32,128,256]{2,1,0:T(8,128)(2,1)}), bf16[32,128,256]{2,1,0:T(8,128)(2,1)S(1)}, u32[]{:S(2)}, u32[]{:S(2)}) async-start(bf16[32,128,256]{2,1,0:T(8,128)(2,1)} %get-tuple-element.14), calls=%async_computation.3 | async-start | bytes 4194304 | tf_op jit(solution)/shard_map/all_to_all | solution.py:223
  189.7 1.3 copy-start.5
  191.1 38.8 %all-to-all-start.2 = ((bf16[32,256,128]{2,1,0:T(8,128)(2,1)}), bf16[32,256,128]{2,1,0:T(8,128)(2,1)S(1)}, u32[]{:S(2)}, u32[]{:S(2)}) async-start(bf16[32,256,128]{2,1,0:T(8,128)(2,1)} %bitcast.56), calls=%async_computation.2 | async-start | bytes 4194304 | tf_op jit(solution)/shard_map/all_to_all | solution.py:223
  197.8 185.2 %all-gather.9.cloned.1.call-start = ((), (), s32[]{:S(2)}) async-start(), calls=%async_computation.9 | async-start | bytes 34603008 | tf_op jit(solution)/shard_map/all_gather | solution.py:253
  229.9 1.3 copy-start.1
  282.7 53.4 %all-to-all-start.4 = ((bf16[32,256,128]{2,1,0:T(8,128)(2,1)}), bf16[32,256,128]{2,1,0:T(8,128)(2,1)S(1)}, u32[]{:S(2)}, u32[]{:S(2)}) async-start(bf16[32,256,128]{2,1,0:T(8,128)(2,1)} %bitcast.55), calls=%async_computation.4 | async-start | bytes 4194304 | tf_op jit(solution)/shard_map/all_to_all | solution.py:223
  289.0 200.6 %all-gather.7.cloned.1.call-start = ((), (), s32[]{:S(2)}) async-start(), calls=%async_computation.8 | async-start | bytes 34603008 | tf_op jit(solution)/shard_map/all_gather | solution.py:253
  336.1 1.3 copy-start
  337.4 20.0 %copy-start.10 = (f32[128,256]{1,0:T(8,128)S(1)}, f32[128,256]{1,0:T(8,128)}, u32[]{:S(2)}) copy-start(f32[128,256]{1,0:T(8,128)} %get-tuple-element.21) | copy-start | bytes 393220
  350.4 21.8 %copy-start.6 = (bf16[256,2048]{1,0:T(8,128)(2,1)S(1)}, bf16[256,2048]{1,0:T(8,128)(2,1)}, u32[]{:S(2)}) copy-start(bf16[256,2048]{1,0:T(8,128)(2,1)} %get-tuple-element.15.rest_0_) | copy-start | bytes 3145732
  350.4 21.8 %copy-start.7 = (bf16[256,2048]{1,0:T(8,128)(2,1)S(1)}, bf16[256,2048]{1,0:T(8,128)(2,1)}, u32[]{:S(2)}) copy-start(bf16[256,2048]{1,0:T(8,128)(2,1)} %get-tuple-element.16) | copy-start | bytes 3145732
  350.5 18.4 %all-to-all-start.5 = ((f32[32,2,4,256]{3,2,1,0:T(4,128)}), f32[32,2,4,256]{3,2,1,0:T(4,128)S(1)}, u32[]{:S(2)}, u32[]{:S(2)}) async-start(f32[32,2,4,256]{3,2,1,0:T(4,128)} %bitcast.54), calls=%async_computation.5 | async-start | bytes 524288 | tf_op jit(solution)/shard_map/all_to_all | solution.py:223
  368.9 4.9 copy-start.2
  368.9 11.2 %all-to-all-start.7 = ((f32[32,4,256]{2,1,0:T(4,128)}), f32[32,4,256]{2,1,0:T(4,128)S(1)}, u32[]{:S(2)}, u32[]{:S(2)}) async-start(f32[32,4,256]{2,1,0:T(4,128)} %reshape.24), calls=%async_computation.7 | async-start | bytes 262144 | tf_op jit(solution)/shard_map/all_to_all | solution.py:223
  372.2 1.5 copy-start.11
  380.1 2.9 copy-start.8
  380.1 24.7 %all-to-all-start.6 = ((f32[32,4,256]{2,1,0:T(4,128)}), f32[32,4,256]{2,1,0:T(4,128)S(1)}, u32[]{:S(2)}, u32[]{:S(2)}) async-start(f32[32,4,256]{2,1,0:T(4,128)} %reshape.23), calls=%async_computation.6 | async-start | bytes 262144 | tf_op jit(solution)/shard_map/all_to_all | solution.py:223
  404.8 84.8 %copy-start.9 = (f32[32,4,256]{2,1,0:T(4,128)}, f32[32,4,256]{2,1,0:T(4,128)S(1)}, u32[]{:S(2)}) copy-start(f32[32,4,256]{2,1,0:T(4,128)S(1)} %all-to-all-done.6.gate_ref) | copy-start | bytes 393220
Sparse Core Ops, SparseCore 0:
  68.1 54.0 all-gather.10
  123.8 47.1 all-gather.12
  244.4 135.1 all-gather.8
  381.6 107.9 all-gather.6

commit v4 on v3

--- a/solution.py
+++ b/solution.py
@@ -2,6 +2,7 @@
 import math
 import jax
 import jax.numpy as jnp
+from jax.experimental.layout import Layout, with_layout_constraint
 from jax import lax
 from jax.experimental import pallas as pl
 from jax.experimental.pallas import tpu as pltpu
@@ -227,6 +228,7 @@
         ranks = slot_ranks(expert_ids, experts, cap).reshape(n_micro, groups, own, tok).transpose(1, 0, 2, 3)
         mine = swap(kv, axis_index_groups=columns)
         queries = jnp.einsum('mtd,dhk->hmkt', tokens, w_query, preferred_element_type=F32).astype(BF16)
+        queries = with_layout_constraint(queries, Layout(major_to_minor=(0, 1, 2, 3)))
         mine, queries, ranks = lax.optimization_barrier((mine, queries, ranks))
         ranks = swap(ranks)
         kv_held, q_held = [], []

time: 519 us -> 496 us (0.956)
  local copies, waits for them, and re-layouts: 47.1 us -> 23.1 us
    unnamed x31 -> x30, local copies, waits for them, and re-layouts: 36.5 us -> 12.5 us
  transfers between devices with their start and end apart: 11 -> 11, of which waited for: 4 -> 4; matrix products, arithmetic and copies ran while one was open for 10% -> 6% of each run, Pallas kernels for 32% -> 33%
where the time goes in v4:
time: 496 us; the launch traced here: 495 us
  Pallas kernels  200 us (40%)
  waiting for transfers between devices  148 us (30%)
  blocking collectives  49.3 us (10%)
  starting transfers between devices  37.2 us (8%)
  local copies, waits for them, and re-layouts  23.1 us (5%)
  matrix products  21.9 us (4%)
  between operations  13.9 us (3%)
    pallas_call x3, Pallas kernels, attention(): pl.pallas_call(functools.partial(attention_kernel, lo), grid=(hi - lo,),...  130 us
    all_gather x2, waiting for transfers between devices, local_step(): lax.all_gather(piece, 'sp', axis=0, tiled=True)  84.8 us
    all_to_all x7, waiting for transfers between devices, swap(): return lax.all_to_all(a, 'sp', 0, 0, tiled=True, **kw)  62.4 us
    all_to_all x1, blocking collectives, swap(): return lax.all_to_all(a, 'sp', 0, 0, tiled=True, **kw)  49.3 us
    pallas_call x2, Pallas kernels, expert_rows(): pl.pallas_call(rows_kernel, grid=(sources // some,), in_specs=[pl.BlockSp...  43.5 us
    all_to_all x7, starting transfers between devices, swap(): return lax.all_to_all(a, 'sp', 0, 0, tiled=True, **kw)  36.8 us
    pallas_call x2, Pallas kernels, project(): pl.pallas_call(functools.partial(project_kernel, heads_blk, parts), grid=...  26.1 us
    dot_general x1, matrix products, local_step(): jnp.einsum('mtd,dhk->hmkt', tokens, w_query, preferred_element_type=F32)  15.4 us
  transfers between devices with their start and end apart: 11, of which 4 were waited for; matrix products, arithmetic and copies ran while one was open for 6% of the time, Pallas kernels for 33%

profile of v4, /device:TPU:97, one launch (start us, length us, event | category | flops | bytes accessed | tf_op | source)
XLA Modules:
  0.0 495.4 jit_solution(16899972837036601738)
XLA Ops:
  7.2 4.4 copy.39
  11.6 2.6 copy.40
  14.1 6.2 %fusion.13 = bf16[4,2,256,256]{3,2,1,0:T(8,128)(2,1)} fusion(bf16[2,256,2048]{2,1,0:T(8,128)(2,1)} %param.7, bf16[2048,4,128]{0,2,1:T(8,128)(2,1)} %copy.40, bf16[2048,4,128]{0,2,1:T(8,128)(2,1)} %copy.39), kind=kOutput, calls=%fused_computation.15 | convolution fusion | flops 2156396544 | bytes 7340032 | tf_op jit(solution)/shard_map/mtd,dhk->hmkt/dot_general | solution.py:227
  20.4 6.6 %all-to-all-start = ((bf16[4,2,256,256]{3,2,1,0:T(8,128)(2,1)}), bf16[4,2,256,256]{3,2,1,0:T(8,128)(2,1)S(1)}, u32[]{:S(2)}, u32[]{:S(2)}) async-start(bf16[4,2,256,256]{3,2,1,0:T(8,128)(2,1)} %fusion.13), calls=%async_computation | async-start | bytes 2097152 | tf_op jit(solution)/shard_map/all_to_all | solution.py:224
  27.0 15.4 %convert_bitcast_fusion = bf16[32,2,128,256]{3,2,1,0:T(8,128)(2,1)} fusion(bf16[2048,32,128,1]{2,1,0,3:T(8,128)(2,1)} %bitcast.56, bf16[2,256,2048]{2,1,0:T(8,128)(2,1)S(1)} %copy-done.4), kind=kOutput, calls=%fused_computation.6 | convolution fusion | flops 8592031744 | bytes 23068672 | tf_op jit(solution)/shard_map/mtd,dhk->hmkt/dot_general | solution.py:230
  42.4 0.8 fusion.9
  43.2 0.2 and_select_fusion
  43.5 0.2 copy.42
  43.7 0.8 copy.61
  44.4 1.1 fusion.22
  45.5 0.1 all-gather.11.cloned.1.call-update
  45.6 0.1 all-gather.13.cloned.1.call-start
  45.6 0.7 all-gather.13.cloned.1.call-update
  46.4 4.0 slice_bitcast_fusion.1
  50.4 49.3 %all_to_all.40.q_ref = bf16[32,128,256]{2,1,0:T(8,128)(2,1)} all-to-all(bf16[32,128,256]{2,1,0:T(8,128)(2,1)S(1)} %get-tuple-element.22), channel_id=1, replica_groups=mesh['dp'=1,'sp'=32] {'sp'}, dimensions={0} | all-to-all | bytes 4194304 | tf_op jit(solution)/shard_map/all_to_all | solution.py:224
  99.7 4.1 all-to-all-start.3
  103.8 0.0 all-gather.11.cloned.1.call-done
  103.8 63.5 %attend.3 = bf16[8192,128]{1,0:T(8,128)(2,1)} custom-call(bf16[32,128,256]{2,1,0:T(8,128)(2,1)} %all_to_all.40.q_ref, bf16[8,4,256,256]{3,2,1,0:T(8,128)(2,1)} %bitcast.59), custom_call_target="tpu_custom_call" | custom-call | flops 34359738368 | bytes 8388608 | tf_op jit(solution)/shard_map/attend/pallas_call | solution.py:74
  167.3 0.0 all-to-all-done.3.q_ref
  167.3 1.3 copy-done.5
  168.6 6.7 %all-to-all-start.2 = ((bf16[32,256,128]{2,1,0:T(8,128)(2,1)}), bf16[32,256,128]{2,1,0:T(8,128)(2,1)S(1)}, u32[]{:S(2)}, u32[]{:S(2)}) async-start(bf16[32,256,128]{2,1,0:T(8,128)(2,1)} %bitcast.50), calls=%async_computation.2 | async-start | bytes 4194304 | tf_op jit(solution)/shard_map/all_to_all | solution.py:224
  175.3 0.1 all-gather.9.cloned.1.call-start
  175.4 0.8 copy.52
  176.2 3.1 slice_bitcast_fusion.2
  179.3 28.1 %attend.4.rest_0_.rest_1_ = bf16[8192,128]{1,0:T(8,128)(2,1)} custom-call(bf16[32,128,256]{2,1,0:T(8,128)(2,1)} %copy-done.5, bf16[8,4,256,256]{3,2,1,0:T(8,128)(2,1)} %bitcast.57), custom_call_target="tpu_custom_call" | custom-call | flops 13421772800 | bytes 8388608 | tf_op jit(solution)/shard_map/attend/pallas_call | solution.py:74
  207.4 1.3 copy-done.1
  208.8 13.1 %project.2 = (bf16[256,2048]{1,0:T(8,128)(2,1)}, bf16[256,2048]{1,0:T(8,128)(2,1)}, f32[128,256]{1,0:T(8,128)}) custom-call(bf16[32,256,128]{2,1,0:T(8,128)(2,1)} %copy-done.1, bf16[32,128,2048]{2,1,0:T(8,128)(2,1)} %w_ref.3, bf16[256,2048]{1,0:T(8,128)(2,1)} %get-tuple-element.25.x_ref, s32[256,8]{1,0:T(8,128)} %bitcast.54, bf16[2048,128]{1,0:T(8,128)(2,1)} %wr_ref.3, ...), custom_call_target="tpu_custom_call" | custom-call | flops 4294967296 | bytes 16777216 | tf_op jit(solution)/shard_map/project/pallas_call | solution.py:131
  221.8 0.1 all-gather.9.cloned.1.call-update
  221.9 38.4 %attend.5.rest_0_ = bf16[8192,128]{1,0:T(8,128)(2,1)} custom-call(bf16[32,128,256]{2,1,0:T(8,128)(2,1)} %copy-done.5, bf16[8,4,256,256]{3,2,1,0:T(8,128)(2,1)} %bitcast.58, bf16[256,2048]{1,0:T(8,128)(2,1)} %get-tuple-element.15.rest_0_, bf16[8192,128]{1,0:T(8,128)(2,1)} %attend.4.rest_0_.rest_1_), custom_call_target="tpu_custom_call", output_to_operand_aliasing={{}: (3, {})} | custom-call | flops 20937965568 | bytes 8388608 | tf_op jit(solution)/shard_map/attend/pallas_call | solution.py:74
  260.3 6.3 %all-to-all-start.4 = ((bf16[32,256,128]{2,1,0:T(8,128)(2,1)}), bf16[32,256,128]{2,1,0:T(8,128)(2,1)S(1)}, u32[]{:S(2)}, u32[]{:S(2)}) async-start(bf16[32,256,128]{2,1,0:T(8,128)(2,1)} %bitcast.49), calls=%async_computation.4 | async-start | bytes 4194304 | tf_op jit(solution)/shard_map/all_to_all | solution.py:224
  266.6 0.3 all-gather.7.cloned.1.call-start
  266.9 0.8 copy.53
  267.6 46.0 %all-to-all-done.4.o_ref = bf16[32,256,128]{2,1,0:T(8,128)(2,1)S(1)} async-done(((bf16[32,256,128]{2,1,0:T(8,128)(2,1)}), bf16[32,256,128]{2,1,0:T(8,128)(2,1)S(1)}, u32[]{:S(2)}, u32[]{:S(2)}) %all-to-all-start.4) | async-done | bytes 2097184 | tf_op jit(solution)/shard_map/all_to_all | solution.py:224
  313.7 1.3 copy-done
  315.0 13.0 %project.3 = (bf16[256,2048]{1,0:T(8,128)(2,1)}, bf16[256,2048]{1,0:T(8,128)(2,1)}, f32[128,256]{1,0:T(8,128)}) custom-call(bf16[32,256,128]{2,1,0:T(8,128)(2,1)} %copy-done, bf16[32,128,2048]{2,1,0:T(8,128)(2,1)} %w_ref.3, bf16[256,2048]{1,0:T(8,128)(2,1)} %get-tuple-element.24.x_ref, s32[256,8]{1,0:T(8,128)} %bitcast.55, bf16[2048,128]{1,0:T(8,128)(2,1)} %wr_ref.3), custom_call_target="tpu_custom_call" | custom-call | flops 4294967296 | bytes 16777216 | tf_op jit(solution)/shard_map/project/pallas_call | solution.py:131
  328.0 0.1 all-gather.7.cloned.1.call-update
  328.1 6.9 %all-to-all-start.5 = ((f32[32,2,4,256]{3,2,1,0:T(4,128)}), f32[32,2,4,256]{3,2,1,0:T(4,128)S(1)}, u32[]{:S(2)}, u32[]{:S(2)}) async-start(f32[32,2,4,256]{3,2,1,0:T(4,128)} %bitcast.48), calls=%async_computation.5 | async-start | bytes 524288 | tf_op jit(solution)/shard_map/all_to_all | solution.py:224
  335.0 0.7 reshape.24
  335.7 10.8 %all-to-all-done.5.rank_ref = f32[32,2,4,256]{3,2,1,0:T(4,128)S(1)} async-done(((f32[32,2,4,256]{3,2,1,0:T(4,128)}), f32[32,2,4,256]{3,2,1,0:T(4,128)S(1)}, u32[]{:S(2)}, u32[]{:S(2)}) %all-to-all-start.5) | async-done | bytes 262176 | tf_op jit(solution)/shard_map/all_to_all | solution.py:224
  346.4 3.3 all-to-all-start.7
  349.8 1.5 pad_maximum_fusion
  351.3 0.7 reshape.23
  352.0 5.7 %all-to-all-done.7.gate_ref = f32[32,4,256]{2,1,0:T(4,128)S(1)} async-done(((f32[32,4,256]{2,1,0:T(4,128)}), f32[32,4,256]{2,1,0:T(4,128)S(1)}, u32[]{:S(2)}, u32[]{:S(2)}) %all-to-all-start.7) | async-done | bytes 131104 | tf_op jit(solution)/shard_map/all_to_all | solution.py:224
  357.7 2.9 all-to-all-start.6
  360.5 0.0 all-gather.9.cloned.1.call-done.h_ref
  360.6 21.8 %expert_rows.2.rest_0_ = bf16[2,4,1024,2048]{3,2,1,0:T(8,128)(2,1)} custom-call(bf16[8192,2048]{1,0:T(8,128)(2,1)} %all-gather.9.cloned.1.call-done.h_ref, f32[32,2,4,256]{3,2,1,0:T(4,128)} %copy-done.2, f32[32,4,256]{2,1,0:T(4,128)} %copy-done.8, bf16[8192,128]{1,0:T(8,128)(2,1)} %attend.5.rest_0_), custom_call_target="tpu_custom_call" | custom-call | flops 4294967296 | bytes 50331648 | tf_op jit(solution)/shard_map/expert_rows/pallas_call | solution.py:181
  382.3 84.8 %all-gather.7.cloned.1.call-done.h_ref = bf16[8192,2048]{1,0:T(8,128)(2,1)} async-done(((bf16[256,2048]{1,0:T(8,128)(2,1)}), bf16[8192,2048]{1,0:T(8,128)(2,1)}) %all-gather.7.cloned.1.call-update) | async-done | bytes 33554448 | tf_op jit(solution)/shard_map/all_gather | solution.py:255
  467.2 21.7 %expert_rows.3 = bf16[2,4,1024,2048]{3,2,1,0:T(8,128)(2,1)} custom-call(bf16[8192,2048]{1,0:T(8,128)(2,1)} %all-gather.7.cloned.1.call-done.h_ref, f32[32,2,4,256]{3,2,1,0:T(4,128)} %copy-done.2, f32[32,4,256]{2,1,0:T(4,128)} %copy-done.9, bf16[2,4,1024,2048]{3,2,1,0:T(8,128)(2,1)} %expert_rows.2.rest_0_), custom_call_target="tpu_custom_call", output_to_operand_aliasing={{}: (3, {})} | custom-call | flops 4294967296 | bytes 50331648 | tf_op jit(solution)/shard_map/expert_rows/pallas_call | solution.py:181
  (29 shorter events, 0.1 us)
Async XLA Ops:
  7.2 4.4 copy-start.3
  20.4 6.6 %copy-start.4 = (bf16[2,256,2048]{2,1,0:T(8,128)(2,1)S(1)}, bf16[2,256,2048]{2,1,0:T(8,128)(2,1)}, u32[]{:S(2)}) copy-start(bf16[2,256,2048]{2,1,0:T(8,128)(2,1)} %param.7) | copy-start | bytes 6291460
  20.4 24.1 %all-to-all-start = ((bf16[4,2,256,256]{3,2,1,0:T(8,128)(2,1)}), bf16[4,2,256,256]{3,2,1,0:T(8,128)(2,1)S(1)}, u32[]{:S(2)}, u32[]{:S(2)}) async-start(bf16[4,2,256,256]{3,2,1,0:T(8,128)(2,1)} %fusion.13), calls=%async_computation | async-start | bytes 2097152 | tf_op jit(solution)/shard_map/all_to_all | solution.py:224
  27.0 76.8 %all-gather.11.cloned.1.call-start = ((), (), s32[]{:S(2)}) async-start(), calls=%async_computation.10 | async-start | bytes 4718592 | tf_op jit(solution)/shard_map/all_gather | solution.py:239
  27.0 15.4 %copy-start.12 = (s32[2,256,8]{1,2,0:T(8,128)S(1)}, s32[2,256,8]{1,2,0:T(8,128)}, u32[]{:S(2)}) copy-start(s32[2,256,8]{1,2,0:T(8,128)} %param.8) | copy-start | bytes 49156
  45.6 133.7 %all-gather.13.cloned.1.call-start = ((), (), s32[]{:S(2)}) async-start(), calls=%async_computation.11 | async-start | bytes 4718592 | tf_op jit(solution)/shard_map/all_gather | solution.py:239
  99.7 67.6 %all-to-all-start.3 = ((bf16[32,128,256]{2,1,0:T(8,128)(2,1)}), bf16[32,128,256]{2,1,0:T(8,128)(2,1)S(1)}, u32[]{:S(2)}, u32[]{:S(2)}) async-start(bf16[32,128,256]{2,1,0:T(8,128)(2,1)} %get-tuple-element.14), calls=%async_computation.3 | async-start | bytes 4194304 | tf_op jit(solution)/shard_map/all_to_all | solution.py:224
  167.3 1.3 copy-start.5
  168.6 38.8 %all-to-all-start.2 = ((bf16[32,256,128]{2,1,0:T(8,128)(2,1)}), bf16[32,256,128]{2,1,0:T(8,128)(2,1)S(1)}, u32[]{:S(2)}, u32[]{:S(2)}) async-start(bf16[32,256,128]{2,1,0:T(8,128)(2,1)} %bitcast.50), calls=%async_computation.2 | async-start | bytes 4194304 | tf_op jit(solution)/shard_map/all_to_all | solution.py:224
  175.3 185.2 %all-gather.9.cloned.1.call-start = ((), (), s32[]{:S(2)}) async-start(), calls=%async_computation.9 | async-start | bytes 34603008 | tf_op jit(solution)/shard_map/all_gather | solution.py:255
  207.4 1.3 copy-start.1
  260.3 53.4 %all-to-all-start.4 = ((bf16[32,256,128]{2,1,0:T(8,128)(2,1)}), bf16[32,256,128]{2,1,0:T(8,128)(2,1)S(1)}, u32[]{:S(2)}, u32[]{:S(2)}) async-start(bf16[32,256,128]{2,1,0:T(8,128)(2,1)} %bitcast.49), calls=%async_computation.4 | async-start | bytes 4194304 | tf_op jit(solution)/shard_map/all_to_all | solution.py:224
  266.6 200.6 %all-gather.7.cloned.1.call-start = ((), (), s32[]{:S(2)}) async-start(), calls=%async_computation.8 | async-start | bytes 34603008 | tf_op jit(solution)/shard_map/all_gather | solution.py:255
  313.7 1.3 copy-start
  315.0 20.0 %copy-start.10 = (f32[128,256]{1,0:T(8,128)S(1)}, f32[128,256]{1,0:T(8,128)}, u32[]{:S(2)}) copy-start(f32[128,256]{1,0:T(8,128)} %get-tuple-element.21) | copy-start | bytes 393220
  328.0 21.8 %copy-start.6 = (bf16[256,2048]{1,0:T(8,128)(2,1)S(1)}, bf16[256,2048]{1,0:T(8,128)(2,1)}, u32[]{:S(2)}) copy-start(bf16[256,2048]{1,0:T(8,128)(2,1)} %get-tuple-element.15.rest_0_) | copy-start | bytes 3145732
  328.0 21.8 %copy-start.7 = (bf16[256,2048]{1,0:T(8,128)(2,1)S(1)}, bf16[256,2048]{1,0:T(8,128)(2,1)}, u32[]{:S(2)}) copy-start(bf16[256,2048]{1,0:T(8,128)(2,1)} %get-tuple-element.16) | copy-start | bytes 3145732
  328.1 18.4 %all-to-all-start.5 = ((f32[32,2,4,256]{3,2,1,0:T(4,128)}), f32[32,2,4,256]{3,2,1,0:T(4,128)S(1)}, u32[]{:S(2)}, u32[]{:S(2)}) async-start(f32[32,2,4,256]{3,2,1,0:T(4,128)} %bitcast.48), calls=%async_computation.5 | async-start | bytes 524288 | tf_op jit(solution)/shard_map/all_to_all | solution.py:224
  346.4 4.9 copy-start.2
  346.4 11.2 %all-to-all-start.7 = ((f32[32,4,256]{2,1,0:T(4,128)}), f32[32,4,256]{2,1,0:T(4,128)S(1)}, u32[]{:S(2)}, u32[]{:S(2)}) async-start(f32[32,4,256]{2,1,0:T(4,128)} %reshape.24), calls=%async_computation.7 | async-start | bytes 262144 | tf_op jit(solution)/shard_map/all_to_all | solution.py:224
  349.8 1.5 copy-start.11
  357.7 2.9 copy-start.8
  357.7 24.7 %all-to-all-start.6 = ((f32[32,4,256]{2,1,0:T(4,128)}), f32[32,4,256]{2,1,0:T(4,128)S(1)}, u32[]{:S(2)}, u32[]{:S(2)}) async-start(f32[32,4,256]{2,1,0:T(4,128)} %reshape.23), calls=%async_computation.6 | async-start | bytes 262144 | tf_op jit(solution)/shard_map/all_to_all | solution.py:224
  382.3 84.8 %copy-start.9 = (f32[32,4,256]{2,1,0:T(4,128)}, f32[32,4,256]{2,1,0:T(4,128)S(1)}, u32[]{:S(2)}) copy-start(f32[32,4,256]{2,1,0:T(4,128)S(1)} %all-to-all-done.6.gate_ref) | copy-start | bytes 393220
Sparse Core Ops, SparseCore 0:
  45.7 54.0 all-gather.10
  101.4 47.1 all-gather.12
  222.0 135.1 all-gather.8
  359.1 107.9 all-gather.6
